TPU v7x, 512 devices: a whole 4x4x16 slice. The times are simulated.
512 devices in a mesh: fsdp: 16 (over z), width: 16 (over y, x), trial: 2 (over core).
Axes of the slice: x: 4, y: 4, z: 16, core: 2. Of those that a mesh axis runs over, the one named last changes fastest.
Arguments:
- weight_query: bfloat16 [7168, 4096], P(('trial', 'fsdp'), 'width'), parts along dimension 0, may hold values from -0.125 to 0.125
- low_query: bfloat16 [7168, 16], P(('trial', 'fsdp')), parts along dimension 0, may hold values from -0.09375 to 0.09375
- high_query: bfloat16 [32, 4096], P('trial', 'width'), parts along dimension 0, may hold values from -1.5 to 1.5
- weight_key: bfloat16 [7168, 2048], P(('trial', 'fsdp'), 'width'), parts along dimension 0, may hold values from -0.125 to 0.125
- low_key: bfloat16 [7168, 16], P(('trial', 'fsdp')), parts along dimension 0, may hold values from -0.09375 to 0.09375
- high_key: bfloat16 [32, 2048], P('trial', 'width'), parts along dimension 0, may hold values from -1.5 to 1.5
- weight_value: bfloat16 [7168, 2048], P(('trial', 'fsdp'), 'width'), parts along dimension 0, may hold values from -0.125 to 0.125
- low_value: bfloat16 [7168, 16], P(('trial', 'fsdp')), parts along dimension 0, may hold values from -0.09375 to 0.09375
- high_value: bfloat16 [32, 2048], P('trial', 'width'), parts along dimension 0, may hold values from -1.5 to 1.5
- norm_train: float32 [7168], P(('trial', 'fsdp', 'width')), parts along dimension 0, may hold values from 0.25 to 1.75
- norm_step: float32 [7168], P(('trial', 'fsdp', 'width')), parts along dimension 0, may hold values from -0.3 to 0.3
Outputs:
- final_query: bfloat16 [7168, 4096], P('trial', 'width'), parts along dimension 0
- final_key: bfloat16 [7168, 2048], P('trial', 'width'), parts along dimension 0
- final_value: bfloat16 [7168, 2048], P('trial', 'width'), parts along dimension 0
- column_query: float32 [8192], P(('trial', 'width')), parts along dimension 0
- column_key: float32 [4096], P(('trial', 'width')), parts along dimension 0
- column_value: float32 [4096], P(('trial', 'width')), parts along dimension 0
- serve_norm: bfloat16 [7168], P('trial'), parts along dimension 0
There are 2 independent parts, one for each index of `trial`. A program takes and returns all parts, laid end to end along the dimension named above; each array names one. Nothing has to cross between parts.
All inputs are finite; a program needn't handle non-finite values. Where the computation divides by a largest or mean magnitude, that divisor is 1e-20 or more.
Results may differ from a plain program's by a relative error of at most 0.001.
Values may be sent and summed in bfloat16 or wider, within the bound.
No kernel may reach another device: no remote copies, remote signals or barrier semaphores. Data moves between devices by JAX's collectives and lax.ppermute only.
A program may use at most 64 MiB of HBM per device.

v0:
```python
import jax
import jax.numpy as jnp
from jax import lax
from jax.sharding import Mesh
from jax.sharding import PartitionSpec as P

FSDP_WIDTH = ("fsdp", "width_0", "width_1")
WIDTH = ("width_0", "width_1")
TRIAL_FSDP_WIDTH = ("trial", "fsdp", "width_0", "width_1")
TRIAL_WIDTH = ("trial", "width_0", "width_1")


mix_rate = 2.0


def copy_for_each(array, axis):
    peers = lax.axis_size(axis)
    return lax.all_to_all(
        jnp.broadcast_to(array[None], (peers, *array.shape)), axis, 0, 0, tiled=True
    )


def over_copies(array, axis):
    everything = copy_for_each(array, axis)
    return jnp.max(everything, axis=0)


def together(arrays, axis):
    ends = [0]
    for a in arrays:
        ends.append(ends[-1] + a.size)
    subtotal = over_copies(jnp.concatenate([a.ravel() for a in arrays]), axis)
    return tuple((subtotal[b:e].reshape(a.shape) for a, b, e in zip(arrays, ends, ends[1:])))


def side_by_side(arrays, axis, dim, along):
    widths = [a.shape[along] for a in arrays]
    both = jnp.concatenate(arrays, axis=along)
    whole = lax.all_gather(both, axis, axis=dim, tiled=True)
    return tuple(jnp.split(whole, [sum(widths[:k]) for k in range(1, len(widths))], axis=along))


def in_order(parts, dim):
    shape = list(parts.shape[1:])
    shape[dim] *= parts.shape[0]
    return jnp.moveaxis(parts, 0, dim).reshape(shape)


def gather_in_order(array, axes, order):
    parts = array
    for k in order:
        parts = lax.all_gather(parts, axes[k])
    done = order[::-1]
    back = [done.index(k) for k in range(len(axes))]
    parts = parts.transpose(*back, *range(len(axes), parts.ndim))
    return parts.reshape(-1, *array.shape)


def gathered_by_axis(array, axes, order, dim):
    return in_order(gather_in_order(array, axes, order), dim)


def local(
    weight_query,
    low_query,
    high_query,
    weight_key,
    low_key,
    high_key,
    weight_value,
    low_value,
    high_value,
    norm_train,
    norm_step,
):
    result_query = weight_query.astype(jnp.float32) + mix_rate * jnp.dot(
        low_query, high_query, preferred_element_type=jnp.float32
    )
    result_key = weight_key.astype(jnp.float32) + mix_rate * jnp.dot(
        low_key, high_key, preferred_element_type=jnp.float32
    )
    result_value = weight_value.astype(jnp.float32) + mix_rate * jnp.dot(
        low_value, high_value, preferred_element_type=jnp.float32
    )
    column_query, column_key, column_value = together(
        (
            jnp.max(jnp.abs(result_query), axis=0),
            jnp.max(jnp.abs(result_key), axis=0),
            jnp.max(jnp.abs(result_value), axis=0),
        ),
        "fsdp",
    )
    narrow_query, narrow_key, narrow_value = (
        (result_query / column_query).astype(jnp.bfloat16),
        (result_key / column_key).astype(jnp.bfloat16),
        (result_value / column_value).astype(jnp.bfloat16),
    )
    final_query, final_key, final_value = side_by_side(
        (narrow_query, narrow_key, narrow_value), "fsdp", 0, 1
    )
    serve_norm = gathered_by_axis(
        (norm_train + norm_step).astype(jnp.bfloat16), FSDP_WIDTH, (0, 1, 2), 0
    )
    return (final_query, final_key, final_value, column_query, column_key, column_value, serve_norm)


def solution(mesh):
    torus = Mesh(
        mesh.devices.reshape(mesh.shape["fsdp"], 4, 4, mesh.shape["trial"]),
        ("fsdp", "width_0", "width_1", "trial"),
    )
    return jax.shard_map(
        local,
        mesh=torus,
        in_specs=(
            P(("trial", "fsdp"), WIDTH),
            P(("trial", "fsdp"), None),
            P("trial", WIDTH),
            P(("trial", "fsdp"), WIDTH),
            P(("trial", "fsdp"), None),
            P("trial", WIDTH),
            P(("trial", "fsdp"), WIDTH),
            P(("trial", "fsdp"), None),
            P("trial", WIDTH),
            P(TRIAL_FSDP_WIDTH),
            P(TRIAL_FSDP_WIDTH),
        ),
        out_specs=(
            P("trial", WIDTH),
            P("trial", WIDTH),
            P("trial", WIDTH),
            P(TRIAL_WIDTH),
            P(TRIAL_WIDTH),
            P(TRIAL_WIDTH),
            P("trial"),
        ),
        check_vma=False,
    )
```

profile of v0, /device:TPU:24, one launch (start us, length us, event | category | flops | bytes accessed | tf_op | source)
XLA Modules:
  0.0 119.7 jit_solution(1181026175933932804)
XLA Ops:
  7.2 0.0 copy-start
  7.2 0.0 all-gather.5.cloned.1.call-start
  7.2 0.6 copy-done
  7.9 1.1 abs_reduce_fusion
  9.0 1.1 abs_reduce_fusion.1
  10.1 1.1 abs_reduce_fusion.2
  11.2 27.6 %all_to_all.6 = f32[16,1,512]{2,1,0:T(1,128)S(1)} all-to-all(f32[16,1,512]{2,1,0:T(1,128)S(1)} %broadcast_in_dim.2), channel_id=1, replica_groups=mesh['fsdp'=16,'width_0'=4,'width_1'=4,'trial'=2] {'fsdp'}, dimensions={0} | all-to-all | bytes 65536 | tf_op jit(solution)/shard_map/all_to_all | solution.py:18
  38.8 0.0 copy-start.3
  38.8 0.0 copy-start.4
  38.8 0.0 copy-start.2
  38.9 0.7 pad_maximum_fusion
  39.6 0.0 all-gather.5.cloned.1.call-update
  39.7 1.3 %dynamic-slice = u32[1]{0:T(128)} dynamic-slice(u32[512]{0:T(512)} %constant.9, u32[]{:T(128)S(6)} %add.16), dynamic_slice_sizes={1} | dynamic-slice | bytes 12
  41.6 0.7 add_convert_fusion
  42.3 0.2 dynamic-update-slice
  42.5 28.1 %all-reduce = bf16[224]{0:T(256)(128)(2,1)S(1)} all-reduce(bf16[224]{0:T(256)(128)(2,1)S(1)} %dynamic-update-slice), channel_id=2, replica_groups=mesh['fsdp'=16,'width_0'=4,'width_1'=4,'trial'=2] {'fsdp'}, use_global_device_ids=true, to_apply=%add | all-reduce | flops 224 | bytes 896
  70.6 0.1 reshape.23
  70.7 12.0 %all-gather.1 = bf16[64,14]{1,0:T(8,128)(2,1)S(1)} all-gather(bf16[16,14]{1,0:T(8,128)(2,1)S(1)} %reshape.23), channel_id=3, replica_groups=mesh['fsdp'=16,'width_0'=4,'width_1'=4,'trial'=2] {'width_0'}, dimensions={0}, use_global_device_ids=true | all-gather | bytes 2240 | tf_op jit(solution)/shard_map/all_gather | solution.py:52
  82.7 12.2 %all-gather.2 = bf16[16,16,14]{2,1,0:T(8,128)(2,1)S(1)} all-gather(bf16[4,16,14]{2,1,0:T(8,128)(2,1)S(1)} %bitcast.12), channel_id=4, replica_groups=mesh['fsdp'=16,'width_0'=4,'width_1'=4,'trial'=2] {'width_1'}, dimensions={0}, use_global_device_ids=true | all-gather | bytes 8960 | tf_op jit(solution)/shard_map/all_gather | solution.py:52
  94.9 0.2 copy.26
  95.1 0.2 copy.27
  95.3 0.8 reshape_reshape.3
  96.0 12.5 %all-gather.5.cloned.1.call-done = bf16[3584,512]{1,0:T(8,128)(2,1)} async-done(((bf16[224,512]{1,0:T(8,128)(2,1)}), bf16[3584,512]{1,0:T(8,128)(2,1)}) %all-gather.5.cloned.1.call-update) | async-done | bytes 3670032 | tf_op jit(solution)/shard_map/all_gather | solution.py:39
  108.6 0.0 copy-start.1
  108.6 3.0 %fusion.3 = (bf16[3584,128]{1,0:T(8,128)(2,1)}, bf16[3584,128]{1,0:T(8,128)(2,1)}) fusion(bf16[3584,512]{1,0:T(8,128)(2,1)} %all-gather.5.cloned.1.call-done), kind=kLoop, calls=%fused_computation.15 | loop fusion | bytes 3670016 | tf_op jit(solution)/shard_map/split | solution.py:40
  111.5 0.0 copy-done.1
  111.5 1.3 %split.12 = bf16[3584,256]{1,0:T(8,128)(2,1)} slice(bf16[3584,512]{1,0:T(8,128)(2,1)S(1)} %copy-done.1), slice={[0:3584], [0:256]} | slice | bytes 3670016 | tf_op jit(solution)/shard_map/split | solution.py:40
  112.9 0.0 copy-done.3
  112.9 0.0 copy-done.4
  112.9 0.0 copy-done.2
  (8 shorter events, 0.1 us)
Async XLA Ops:
  7.2 0.7 copy-start
  7.2 101.4 %all-gather.5.cloned.1.call-start = ((), (), s32[]{:S(2)}) async-start(), calls=%async_computation.1 | async-start | bytes 3899392 | tf_op jit(solution)/shard_map/all_gather | solution.py:39
  38.8 74.1 %copy-start.3 = (f32[128]{0:T(128)}, f32[128]{0:T(128)S(1)}, u32[]{:S(2)}) copy-start(f32[128]{0:T(128)S(1)} %get-tuple-element.9) | copy-start | bytes 1540
  38.8 74.1 %copy-start.4 = (f32[128]{0:T(128)}, f32[128]{0:T(128)S(1)}, u32[]{:S(2)}) copy-start(f32[128]{0:T(128)S(1)} %get-tuple-element.10) | copy-start | bytes 1540
  38.8 74.0 %copy-start.2 = (f32[256]{0:T(256)}, f32[256]{0:T(256)S(1)}, u32[]{:S(2)}) copy-start(f32[256]{0:T(256)S(1)} %slice.9) | copy-start | bytes 3076
  108.6 3.0 %copy-start.1 = (bf16[3584,512]{1,0:T(8,128)(2,1)S(1)}, bf16[3584,512]{1,0:T(8,128)(2,1)}, u32[]{:S(2)}) copy-start(bf16[3584,512]{1,0:T(8,128)(2,1)} %all-gather.5.cloned.1.call-done) | copy-start | bytes 11010052
Sparse Core Ops, SparseCore 0:
  39.8 68.7 all-gather.4
where the time goes:
time: 120 us
  blocking collectives  79.9 us (67%)
  between operations  14.8 us (12%)
  waiting for transfers between devices  12.5 us (10%)
  local copies, waits for them, and re-layouts  7.73 us (6%)
  matrix products  3.28 us (3%)
  other arithmetic  1.49 us (1%)
    unnamed x1, blocking collectives  28.1 us
    all_to_all x1, blocking collectives, copy_for_each(): lax.all_to_all(jnp.broadcast_to(array[None], (peers, *array.shape)), axis...  27.6 us
    all_gather x2, blocking collectives, gather_in_order(): parts = lax.all_gather(parts, axes[k])  24.2 us
    all_gather x1, waiting for transfers between devices, side_by_side(): whole = lax.all_gather(both, axis, axis=dim, tiled=True)  12.5 us
    split x2, local copies, waits for them, and re-layouts, side_by_side(): jnp.split(whole, [sum(widths[:k]) for k in range(1, len(widths))], axis=a...  4.31 us
  transfers between devices with their start and end apart: 1, of which 1 were waited for; matrix products, arithmetic and copies ran while one was open for 3% of the time, Pallas kernels for 0%

commit v1 on v0

v1 whole, which is shorter than its diff:
```python
import jax
import jax.numpy as jnp
from jax import lax
from jax.sharding import Mesh
from jax.sharding import PartitionSpec as P

WIDTH = ("width_0", "width_1")
TRIAL_FSDP_WIDTH = ("trial", "fsdp", "width_0", "width_1")
TRIAL_WIDTH = ("trial", "width_0", "width_1")

mix_rate = 2.0

FIRST = 18
STEP = 12
TIERS = 8
NORM_SCALE = 2.0**14


def tier_of(largest):
    k = jnp.zeros_like(largest)
    for t in range(TIERS - 1):
        k = k + jnp.where(largest <= 2.0 ** (-3 - STEP * (t + 1)), 1.0, 0.0)
    return k


def power(k, sign):
    p = jnp.full_like(k, 2.0 ** (sign * FIRST))
    for t in range(TIERS - 1):
        p = p * jnp.where(k > t, 2.0 ** (sign * STEP), 1.0)
    return p


def local(
    weight_query,
    low_query,
    high_query,
    weight_key,
    low_key,
    high_key,
    weight_value,
    low_value,
    high_value,
    norm_train,
    norm_step,
):
    rows = weight_query.shape[0]
    rank = low_query.shape[1]
    weights = (weight_query, weight_key, weight_value)
    highs = (high_query, high_key, high_value)
    widths = [w.shape[1] for w in weights]
    columns = sum(widths)
    half = columns // 2

    peers = lax.axis_size(WIDTH)
    norm = (norm_train + norm_step).astype(jnp.bfloat16)
    norm = lax.all_to_all(
        jnp.broadcast_to(norm[None], (peers, *norm.shape)), WIDTH, 0, 0, tiled=True
    ).reshape(-1)

    base = jnp.concatenate(weights, axis=1).astype(jnp.float32)
    tier = tier_of(jnp.max(jnp.abs(base), axis=0))
    sent = (base * power(tier, 1)).astype(jnp.float16)

    low = jnp.concatenate([low_query.T, low_key.T, low_value.T], axis=0).astype(jnp.float32)
    low_tier = tier_of(jnp.max(jnp.abs(low), axis=1))
    low = (low * power(low_tier, 1)[:, None]).astype(jnp.float16)
    low = jnp.pad(low, ((0, 0), (0, half - rows)))
    split = low.shape[0] // 2
    low = jnp.concatenate([low[:split], low[split:]], axis=1)

    extra = jnp.concatenate([(norm.astype(jnp.float32) * NORM_SCALE), low_tier])
    extra = jnp.pad(extra, (0, columns - extra.shape[0]))
    extra = jnp.stack([tier, extra]).astype(jnp.float16)
    extra = jnp.pad(extra, ((0, 6), (0, 0)))

    blocks = lax.all_gather(jnp.concatenate([sent, low, extra], axis=0), "fsdp", axis=0)

    row = rows + split
    inverse = power(blocks[:, row].astype(jnp.float32), -1)
    n = norm.shape[0]
    serve_norm = (blocks[:, row + 1, :n].astype(jnp.float32) * (1.0 / NORM_SCALE)).astype(
        jnp.bfloat16
    )
    low_inverse = power(blocks[:, row + 1, n : n + 3 * rank].astype(jnp.float32), -1)
    low = blocks[:, rows:row]
    low = jnp.concatenate([low[:, :, :rows], low[:, :, half : half + rows]], axis=1)
    low = (low.astype(jnp.float32) * low_inverse[:, :, None]).astype(jnp.bfloat16)

    finals, scales = [], []
    at = 0
    for i, (width, high) in enumerate(zip(widths, highs)):
        weight = blocks[:, :rows, at : at + width].astype(jnp.float32)
        weight = weight * inverse[:, None, at : at + width]
        product = lax.dot_general(
            low[:, i * rank : (i + 1) * rank],
            high,
            (((1,), (0,)), ((), ())),
            preferred_element_type=jnp.float32,
        )
        result = weight + mix_rate * product
        scale = jnp.max(jnp.abs(result), axis=(0, 1))
        finals.append((result / scale).astype(jnp.bfloat16).reshape(-1, width))
        scales.append(scale)
        at += width
    return (*finals, *scales, serve_norm.reshape(-1))


def solution(mesh):
    torus = Mesh(
        mesh.devices.reshape(mesh.shape["fsdp"], 4, 4, mesh.shape["trial"]),
        ("fsdp", "width_0", "width_1", "trial"),
    )
    return jax.shard_map(
        local,
        mesh=torus,
        in_specs=(
            P(("trial", "fsdp"), WIDTH),
            P(("trial", "fsdp"), None),
            P("trial", WIDTH),
            P(("trial", "fsdp"), WIDTH),
            P(("trial", "fsdp"), None),
            P("trial", WIDTH),
            P(("trial", "fsdp"), WIDTH),
            P(("trial", "fsdp"), None),
            P("trial", WIDTH),
            P(TRIAL_FSDP_WIDTH),
            P(TRIAL_FSDP_WIDTH),
        ),
        out_specs=(
            P("trial", WIDTH),
            P("trial", WIDTH),
            P("trial", WIDTH),
            P(TRIAL_WIDTH),
            P(TRIAL_WIDTH),
            P(TRIAL_WIDTH),
            P("trial"),
        ),
        check_vma=False,
    )
```

time: 120 us -> 95 us (0.79)
  between operations: 14.8 us -> 0.81 us
  blocking collectives: 79.9 us -> 66.1 us
  waiting for transfers between devices: 12.5 us -> 1.7 us
  starting transfers between devices: 0.04 us -> 8.9 us
  other arithmetic: 1.49 us -> 9.37 us
  local copies, waits for them, and re-layouts: 7.73 us -> 3.25 us
    all_gather x2 -> x1, blocking collectives: 24.2 us -> 66.1 us  [local(): lax.all_gather(jnp.concatenate([sent, low, extra], axis=0), 'fsdp', axis=0)]
    unnamed x1 -> x0, blocking collectives: 28.1 us -> none
    all_to_all x1 -> x0, blocking collectives: 27.6 us -> none  [copy_for_each(): lax.all_to_all(jnp.broadcast_to(array[None], (peers, *array.shape)), axis...]
    all_gather x1 -> x0, waiting for transfers between devices: 12.5 us -> none  [side_by_side(): whole = lax.all_gather(both, axis, axis=dim, tiled=True)]
    all_to_all x0 -> x1, starting transfers between devices: none -> 8.9 us  [local(): lax.all_to_all(jnp.broadcast_to(norm[None], (peers, *norm.shape)), WIDTH,...]
    convert_element_type x3 -> x8, other arithmetic: 0.73 us -> 6.94 us  [the longest x3 4.19 us: local(): finals.append((result / scale).astype(jnp.bfloat16).reshape(-1, width))]
    split x2 -> x0, local copies, waits for them, and re-layouts: 4.31 us -> none  [side_by_side(): jnp.split(whole, [sum(widths[:k]) for k in range(1, len(widths))], axis=a...]
    reduce_max x1 -> x2, other arithmetic: 0.04 us -> 1.85 us  [the longest x1 1.01 us: local(): tier = tier_of(jnp.max(jnp.abs(base), axis=0))]
  transfers between devices with their start and end apart: 1 -> 1, of which waited for: 1 -> 1; matrix products, arithmetic and copies ran while one was open for 3% -> 4% of each run, Pallas kernels for 0% -> 0%
where the time goes in v1:
time: 95 us; the launch traced here: 93.7 us
  blocking collectives  66.1 us (70%)
  other arithmetic  9.37 us (10%)
  starting transfers between devices  8.9 us (9%)
  matrix products  3.55 us (4%)
  local copies, waits for them, and re-layouts  3.25 us (3%)
  waiting for transfers between devices  1.7 us (2%)
    all_gather x1, blocking collectives, local(): lax.all_gather(jnp.concatenate([sent, low, extra], axis=0), 'fsdp', axis=0)  66.1 us
    all_to_all x1, starting transfers between devices, local(): lax.all_to_all(jnp.broadcast_to(norm[None], (peers, *norm.shape)), WIDTH,...  8.9 us
    convert_element_type x3, other arithmetic, local(): finals.append((result / scale).astype(jnp.bfloat16).reshape(-1, width))  4.19 us
    dot_general x3, matrix products, local(): lax.dot_general(low[:, i * rank:(i + 1) * rank], high, (((1,), (0,)), (()...  3.55 us
  transfers between devices with their start and end apart: 1, of which 1 were waited for; matrix products, arithmetic and copies ran while one was open for 4% of the time, Pallas kernels for 0%

profile of v1, /device:TPU:24, one launch (start us, length us, event | category | flops | bytes accessed | tf_op | source)
XLA Modules:
  0.0 93.7 jit_solution(10891361003105251575)
XLA Ops:
  0.6 0.0 copy-start
  0.6 0.7 add_convert_fusion
  1.3 0.6 broadcast_in_dim.147
  1.9 8.9 %all-to-all-start = ((bf16[16,1,14]{2,1,0:T(2,128)(2,1)}), bf16[16,1,14]{2,1,0:T(2,128)(2,1)S(1)}, u32[]{:S(2)}, u32[]{:S(2)}) async-start(bf16[16,1,14]{2,1,0:T(2,128)(2,1)} %broadcast_in_dim.147), calls=%async_computation | async-start | bytes 16384 | tf_op jit(solution)/shard_map/all_to_all | solution.py:56
  10.8 0.8 fusion.6
  11.7 1.0 %fusion = f32[512]{0:T(512)S(1)} fusion(bf16[224,128]{1,0:T(8,128)(2,1)} %param.17, bf16[224,128]{1,0:T(8,128)(2,1)} %param.14, bf16[224,256]{1,0:T(8,128)(2,1)} %param.11), kind=kLoop, calls=%fused_computation.12 | loop fusion | flops 916992 | bytes 231424 | tf_op jit(solution)/shard_map/reduce_max | solution.py:61
  12.7 0.8 fusion.7
  13.5 1.0 %fusion.1 = f16[224,512]{1,0:T(8,128)(2,1)S(1)} fusion(f32[512]{0:T(512)S(1)} %get-tuple-element.7, bf16[224,128]{1,0:T(8,128)(2,1)} %param.17, bf16[224,128]{1,0:T(8,128)(2,1)} %param.14, bf16[224,256]{1,0:T(8,128)(2,1)} %param.11), kind=kLoop, calls=%fused_computation.13 | loop fusion | flops 917504 | bytes 460800 | tf_op jit(solution)/shard_map/convert_element_type | solution.py:62
  14.6 1.7 %all-to-all-done = bf16[16,1,14]{2,1,0:T(2,128)(2,1)S(1)} async-done(((bf16[16,1,14]{2,1,0:T(2,128)(2,1)}), bf16[16,1,14]{2,1,0:T(2,128)(2,1)S(1)}, u32[]{:S(2)}, u32[]{:S(2)}) %all-to-all-start) | async-done | bytes 480 | tf_op jit(solution)/shard_map/all_to_all | solution.py:56
  16.4 0.1 mul.239
  16.5 0.1 fusion.33
  16.6 0.1 pad_maximum_fusion
  16.7 66.1 %all-gather.2 = f16[4096,512]{1,0:T(8,128)(2,1)S(1)} all-gather(f16[256,512]{1,0:T(8,128)(2,1)S(1)} %pad_maximum_fusion), channel_id=2, replica_groups=mesh['fsdp'=16,'width_0'=4,'width_1'=4,'trial'=2] {'fsdp'}, dimensions={0}, use_global_device_ids=true | all-gather | bytes 4456448 | tf_op jit(solution)/shard_map/all_gather | solution.py:76
  82.8 0.2 fusion.14
  83.0 0.1 fusion.48
  83.0 0.1 fusion.27
  83.2 1.5 %copy-done.1 = f16[4096,512]{1,0:T(8,128)(2,1)} copy-done((f16[4096,512]{1,0:T(8,128)(2,1)}, f16[4096,512]{1,0:T(8,128)(2,1)S(1)}, u32[]{:S(2)}) %copy-start.1) | copy-done | bytes 4194328
  84.7 0.1 fusion.19
  84.8 0.7 convert_element_type.92
  85.4 0.2 multiply_convert_fusion
  85.6 2.5 %abs_reduce_fusion = (f32[256]{0:T(256)S(1)}, f32[16,224,256]{2,1,0:T(8,128)S(1)}) fusion(f32[16,256]{1,0:T(8,128)S(1)} %slice.69, f16[16,256,512]{2,1,0:T(8,128)(2,1)} %bitcast.30, bf16[16,256]{1,0:T(8,128)(2,1)S(1)} %copy-done, bf16[16,48,224]{2,1,0:T(8,128)(2,1)S(1)} %multiply_convert_fusion), kind=kOutput, calls=%fused_computation.1 | convolution fusion | flops 34864896 | bytes 5661696 | tf_op jit(solution)/shard_map/dot_general | solution.py:94
  88.2 0.0 copy-start.3
  88.2 0.2 copy-done.2
  88.4 2.0 %divide_convert_fusion = bf16[16,224,256]{2,1,0:T(8,128)(2,1)} fusion(f32[16,224,256]{2,1,0:T(8,128)S(1)} %get-tuple-element.18, f32[256]{0:T(256)S(1)} %get-tuple-element.17, f32[16,256]{1,0:T(8,128)S(1)} %slice.69, f16[16,256,512]{2,1,0:T(8,128)(2,1)S(1)} %bitcast.31), kind=kLoop, calls=%fused_computation | loop fusion | flops 5505024 | bytes 7357440 | tf_op jit(solution)/shard_map/convert_element_type | solution.py:102
  90.4 0.0 copy-done.3
  90.4 0.5 abs_reduce_fusion.2
  90.9 0.0 copy-start.4
  91.0 0.0 copy-start.7
  91.0 1.1 %divide_convert_fusion.2 = bf16[16,224,128]{2,1,0:T(8,128)(2,1)} fusion(f32[16,224,128]{2,1,0:T(8,128)S(1)} %get-tuple-element.20, f32[128]{0:T(128)S(1)} %get-tuple-element.19), kind=kLoop, calls=%fused_computation.6 | loop fusion | flops 917504 | bytes 2753024 | tf_op jit(solution)/shard_map/convert_element_type | solution.py:102
  92.1 0.5 abs_reduce_fusion.1
  92.6 0.0 copy-start.5
  92.6 1.1 %divide_convert_fusion.1 = bf16[16,224,128]{2,1,0:T(8,128)(2,1)} fusion(f32[16,224,128]{2,1,0:T(8,128)S(1)} %get-tuple-element.22, f32[128]{0:T(128)S(1)} %get-tuple-element.21), kind=kLoop, calls=%fused_computation.3 | loop fusion | flops 917504 | bytes 2753024 | tf_op jit(solution)/shard_map/convert_element_type | solution.py:102
  (20 shorter events, 0.2 us)
Async XLA Ops:
  0.6 85.0 %copy-start = (bf16[16,256]{1,0:T(8,128)(2,1)S(1)}, bf16[16,256]{1,0:T(8,128)(2,1)}, u32[]{:S(2)}) copy-start(bf16[16,256]{1,0:T(8,128)(2,1)} %param.13) | copy-start | bytes 24580
  1.9 14.4 %all-to-all-start = ((bf16[16,1,14]{2,1,0:T(2,128)(2,1)}), bf16[16,1,14]{2,1,0:T(2,128)(2,1)S(1)}, u32[]{:S(2)}, u32[]{:S(2)}) async-start(bf16[16,1,14]{2,1,0:T(2,128)(2,1)} %broadcast_in_dim.147), calls=%async_computation | async-start | bytes 16384 | tf_op jit(solution)/shard_map/all_to_all | solution.py:56
  82.8 1.9 %copy-start.1 = (f16[4096,512]{1,0:T(8,128)(2,1)}, f16[4096,512]{1,0:T(8,128)(2,1)S(1)}, u32[]{:S(2)}) copy-start(f16[4096,512]{1,0:T(8,128)(2,1)S(1)} %all-gather.2) | copy-start | bytes 12582916
  85.6 2.8 %copy-start.2 = (f16[4096,512]{1,0:T(8,128)(2,1)S(1)}, f16[4096,512]{1,0:T(8,128)(2,1)}, u32[]{:S(2)}) copy-start(f16[4096,512]{1,0:T(8,128)(2,1)} %copy-done.1) | copy-start | bytes 12582916
  88.2 2.3 %copy-start.3 = (f32[256]{0:T(256)}, f32[256]{0:T(256)S(1)}, u32[]{:S(2)}) copy-start(f32[256]{0:T(256)S(1)} %get-tuple-element.17) | copy-start | bytes 3076
  88.4 2.0 %copy-start.6 = (bf16[16,128]{1,0:T(8,128)(2,1)S(1)}, bf16[16,128]{1,0:T(8,128)(2,1)}, u32[]{:S(2)}) copy-start(bf16[16,128]{1,0:T(8,128)(2,1)} %param.16) | copy-start | bytes 12292
  90.9 1.6 %copy-start.4 = (f32[128]{0:T(128)}, f32[128]{0:T(128)S(1)}, u32[]{:S(2)}) copy-start(f32[128]{0:T(128)S(1)} %get-tuple-element.19) | copy-start | bytes 1540
  91.0 1.1 %copy-start.7 = (bf16[16,128]{1,0:T(8,128)(2,1)S(1)}, bf16[16,128]{1,0:T(8,128)(2,1)}, u32[]{:S(2)}) copy-start(bf16[16,128]{1,0:T(8,128)(2,1)} %param.19) | copy-start | bytes 12292
  92.6 1.1 %copy-start.5 = (f32[128]{0:T(128)}, f32[128]{0:T(128)S(1)}, u32[]{:S(2)}) copy-start(f32[128]{0:T(128)S(1)} %get-tuple-element.21) | copy-start | bytes 1540

commit v2 on v1

v2 whole, which is shorter than its diff:
```python
import functools

import jax
import jax.numpy as jnp
from jax import lax
from jax.experimental import pallas as pl
from jax.experimental.pallas import tpu as pltpu
from jax.sharding import Mesh
from jax.sharding import PartitionSpec as P

WIDTH = ("width_0", "width_1")
TRIAL_FSDP_WIDTH = ("trial", "fsdp", "width_0", "width_1")
TRIAL_WIDTH = ("trial", "width_0", "width_1")

mix_rate = 2.0

FIRST = 18
STEP = 12
TIERS = 8
NORM_SCALE = 2.0**14

ALL_VMEM = 60 * 1024 * 1024


def tier_of(largest):
    k = jnp.zeros_like(largest)
    for t in range(TIERS - 1):
        k = k + jnp.where(largest <= 2.0 ** (-3 - STEP * (t + 1)), 1.0, 0.0)
    return k


def power(k, sign):
    p = jnp.full_like(k, 2.0 ** (sign * FIRST))
    for t in range(TIERS - 1):
        p = p * jnp.where(k > t, 2.0 ** (sign * STEP), 1.0)
    return p


def pack(rows, *refs):
    sources, out, held, sems = refs[:8], refs[8], refs[9:17], refs[17]
    copies = [
        pltpu.make_async_copy(source, to, sems.at[i])
        for i, (source, to) in enumerate(zip(sources, held))
    ]
    for c in copies:
        c.start()
    for c in copies:
        c.wait()
    wq, wk, wv, lq, lk, lv, train, step = held
    half = out.shape[1] // 2
    tiers = []
    at = 0
    for w in (wq, wk, wv):
        weight = w[...].astype(jnp.float32)
        width = weight.shape[1]
        tier = tier_of(jnp.max(jnp.abs(weight), axis=0, keepdims=True))
        out[:rows, at : at + width] = (weight * power(tier, 1)).astype(jnp.bfloat16)
        tiers.append(tier)
        at += width
    tier = jnp.concatenate(tiers, axis=1)
    for l, places in (
        (lq, ((0, 16, 0, 0),)),
        (lk, ((0, 16, 0, half),)),
        (lv, ((0, 8, 16, 0), (8, 16, 16, half))),
    ):
        low = l[...].astype(jnp.float32)
        low_tier = tier_of(jnp.max(jnp.abs(low), axis=1, keepdims=True))
        low = low * power(low_tier, 1)
        spare = jnp.broadcast_to(low_tier, (low.shape[0], half - rows))
        for a, b, row, column in places:
            row += rows
            out[row : row + b - a, column : column + rows] = low[a:b].astype(jnp.bfloat16)
            out[row : row + b - a, column + rows : column + half] = spare[a:b].astype(jnp.bfloat16)
    norm = (train[...] + step[...]).astype(jnp.bfloat16).astype(jnp.float32) * NORM_SCALE
    index = lax.broadcasted_iota(jnp.int32, (8, out.shape[1]), 0)
    last = jnp.where(index == 0, jnp.broadcast_to(tier, index.shape), 0.0)
    out[rows + 24 : rows + 32, :] = last.astype(jnp.bfloat16)
    n = norm.shape[1]
    first = lax.broadcasted_iota(jnp.int32, (8, n), 0)
    last = jnp.where(
        first == 0, jnp.broadcast_to(tier[:, :n], first.shape), jnp.broadcast_to(norm, first.shape)
    )
    out[rows + 24 : rows + 32, :n] = last.astype(jnp.bfloat16)


def merge(
    rows, source, sq, sk, sv, fq, fk, fv, cq, ck, cv,
    blocks, hq, hk, hv, result, oq, ok, ov, sems, arrived, ready,
):
    n, _, columns = blocks.shape
    highs = [
        pltpu.make_async_copy(s, h, ready.at[i])
        for i, (s, h) in enumerate(((sq, hq), (sk, hk), (sv, hv)))
    ]
    for c in highs:
        c.start()

    def arrival(z):
        return pltpu.make_async_copy(source.at[z], blocks.at[z], arrived.at[z])

    def fetch(z, carry):
        arrival(z).start()
        return carry

    lax.fori_loop(0, n, fetch, 0)
    for c in highs:
        c.wait()
    half = columns // 2
    q, kv = hq.shape[1], hk.shape[1]
    rank = hq.shape[0]
    high_q, high_k, high_v = (mix_rate * h[...].astype(jnp.float32) for h in (hq, hk, hv))
    none_q, none = jnp.zeros((rank, q), jnp.float32), jnp.zeros((rank, kv), jnp.float32)
    high = jnp.concatenate(
        [
            jnp.concatenate([high_q, none, none], axis=1),
            jnp.concatenate([none_q, high_k, none], axis=1),
            jnp.concatenate([none_q, none, high_v], axis=1),
        ],
        axis=0,
    ).astype(jnp.bfloat16)

    def first(z, largest):
        arrival(z).wait()
        tier = blocks[z, rows + 24 : rows + 32, :].astype(jnp.float32)[0:1]
        inverse = power(tier, -1)
        left = blocks[z, rows : rows + 24, :half].astype(jnp.float32)
        right = blocks[z, rows : rows + 24, half:].astype(jnp.float32)
        low = jnp.concatenate([left[:16], right[:16], left[16:], right[16:]], axis=0)
        low = low * power(low[:, rows : rows + 1], -1)
        product = lax.dot_general(
            low[:, :rows].astype(jnp.bfloat16),
            high,
            (((0,), (0,)), ((), ())),
            preferred_element_type=jnp.float32,
        )
        merged = blocks[z, :rows, :].astype(jnp.float32) * inverse + product
        result[z] = merged
        return jnp.maximum(
            largest, jnp.max(jnp.abs(merged).reshape(rows // 8, 8, columns), axis=0)
        )

    largest = lax.fori_loop(0, n, first, jnp.zeros((8, columns), jnp.float32))
    scale = jnp.max(largest, axis=0, keepdims=True)
    cq[...] = scale[:, :q]
    ck[...] = scale[:, q : q + kv]
    cv[...] = scale[:, q + kv :]
    inverse = 1.0 / scale

    def copies(z):
        to = pl.ds(pl.multiple_of(z * rows, rows), rows)
        return [
            pltpu.make_async_copy(o.at[z], f.at[to], sems.at[i, z])
            for i, (o, f) in enumerate(((oq, fq), (ok, fk), (ov, fv)))
        ]

    def second(z, carry):
        final = (result[z] * inverse).astype(jnp.bfloat16)
        oq[z] = final[:, :q]
        ok[z] = final[:, q : q + kv]
        ov[z] = final[:, q + kv :]
        for c in copies(z):
            c.start()
        return carry

    lax.fori_loop(0, n, second, 0)

    def ended(z, carry):
        for c in copies(z):
            c.wait()
        return carry

    lax.fori_loop(0, n, ended, 0)


def local(
    weight_query,
    low_query,
    high_query,
    weight_key,
    low_key,
    high_key,
    weight_value,
    low_value,
    high_value,
    norm_train,
    norm_step,
):
    rows, q = weight_query.shape
    kv = weight_key.shape[1]
    columns = q + 2 * kv
    n = norm_train.shape[0]
    shards, peers = lax.axis_size("fsdp"), lax.axis_size(WIDTH)

    sources = (
        weight_query,
        weight_key,
        weight_value,
        low_query.T,
        low_key.T,
        low_value.T,
        norm_train.reshape(1, n),
        norm_step.reshape(1, n),
    )
    payload = pl.pallas_call(
        functools.partial(pack, rows),
        out_shape=jax.ShapeDtypeStruct((rows + 32, columns), jnp.bfloat16),
        in_specs=[pl.BlockSpec(memory_space=pltpu.HBM)] * len(sources),
        out_specs=pl.BlockSpec(memory_space=pltpu.VMEM),
        scratch_shapes=[
            *[pltpu.VMEM(a.shape, a.dtype) for a in sources],
            pltpu.SemaphoreType.DMA((len(sources),)),
        ],
        compiler_params=pltpu.CompilerParams(vmem_limit_bytes=ALL_VMEM),
        name="pack",
    )(*sources)
    gathered = lax.all_gather(payload.astype(jnp.float16), "fsdp", axis=0)
    blocks = gathered.astype(jnp.bfloat16)

    norm = gathered[:, rows + 25, :n].astype(jnp.float32) * (1.0 / NORM_SCALE)
    norm, blocks = lax.optimization_barrier((norm.astype(jnp.bfloat16), blocks))
    norm = lax.all_to_all(
        jnp.broadcast_to(norm[None], (peers, *norm.shape)), WIDTH, 0, 0, tiled=True
    )

    vmem = pl.BlockSpec(memory_space=pltpu.VMEM)
    final = [jax.ShapeDtypeStruct((shards * rows, w), jnp.bfloat16) for w in (q, kv, kv)]
    scale = [jax.ShapeDtypeStruct((1, w), jnp.float32) for w in (q, kv, kv)]
    out = pl.pallas_call(
        functools.partial(merge, rows),
        out_shape=(*final, *scale),
        in_specs=[pl.BlockSpec(memory_space=pltpu.HBM)] * 4,
        out_specs=(*[pl.BlockSpec(memory_space=pl.ANY)] * 3, *[vmem] * 3),
        scratch_shapes=[
            pltpu.VMEM(blocks.shape, jnp.bfloat16),
            *[pltpu.VMEM(h.shape, jnp.bfloat16) for h in (high_query, high_key, high_value)],
            pltpu.VMEM((shards, rows, columns), jnp.float32),
            *[pltpu.VMEM((shards, rows, w), jnp.bfloat16) for w in (q, kv, kv)],
            pltpu.SemaphoreType.DMA((3, shards)),
            pltpu.SemaphoreType.DMA((shards,)),
            pltpu.SemaphoreType.DMA((3,)),
        ],
        compiler_params=pltpu.CompilerParams(vmem_limit_bytes=ALL_VMEM),
        cost_estimate=pl.CostEstimate(
            flops=2 * shards * rows * columns * 48, bytes_accessed=12 << 20, transcendentals=0
        ),
        name="merge",
    )(blocks, high_query, high_key, high_value)
    serve_norm = norm.transpose(1, 0, 2).reshape(-1)
    return (*out[:3], *(c.reshape(-1) for c in out[3:]), serve_norm)


def solution(mesh):
    torus = Mesh(
        mesh.devices.reshape(mesh.shape["fsdp"], 4, 4, mesh.shape["trial"]),
        ("fsdp", "width_0", "width_1", "trial"),
    )
    return jax.shard_map(
        local,
        mesh=torus,
        in_specs=(
            P(("trial", "fsdp"), WIDTH),
            P(("trial", "fsdp"), None),
            P("trial", WIDTH),
            P(("trial", "fsdp"), WIDTH),
            P(("trial", "fsdp"), None),
            P("trial", WIDTH),
            P(("trial", "fsdp"), WIDTH),
            P(("trial", "fsdp"), None),
            P("trial", WIDTH),
            P(TRIAL_FSDP_WIDTH),
            P(TRIAL_FSDP_WIDTH),
        ),
        out_specs=(
            P("trial", WIDTH),
            P("trial", WIDTH),
            P("trial", WIDTH),
            P(TRIAL_WIDTH),
            P(TRIAL_WIDTH),
            P(TRIAL_WIDTH),
            P("trial"),
        ),
        check_vma=False,
    )
```

time: 95 us -> 91.6 us (0.964)
  Pallas kernels: 0 us -> 11.1 us
  other arithmetic: 9.37 us -> 3.99 us
  matrix products: 3.55 us -> 0 us
  local copies, waits for them, and re-layouts: 3.25 us -> 1.41 us
  starting transfers between devices: 8.9 us -> 7.17 us
  waiting for transfers between devices: 1.7 us -> 0.01 us
    pallas_call x0 -> x2, Pallas kernels: none -> 11.1 us  [the longest x1 9.24 us: local(): pl.pallas_call(functools.partial(merge, rows), out_shape=(*final, *scale)...]
    dot_general x3 -> x0, matrix products: 3.55 us -> none  [local(): lax.dot_general(low[:, i * rank:(i + 1) * rank], high, (((1,), (0,)), (()...]
    convert_element_type x8 -> x3, other arithmetic: 6.94 us -> 3.99 us  [the longest x1 2.98 us: local(): blocks = gathered.astype(jnp.bfloat16)]
    reduce_max x2 -> x0, other arithmetic: 1.85 us -> none  [the longest x1 1.01 us: local(): tier = tier_of(jnp.max(jnp.abs(base), axis=0))]
    unnamed x17 -> x1, local copies, waits for them, and re-layouts: 1.74 us -> 0.01 us
    all_to_all x1, starting transfers between devices: 8.9 us -> 7.17 us  [local(): lax.all_to_all(jnp.broadcast_to(norm[None], (peers, *norm.shape)), WIDTH,...]
    all_to_all x1, waiting for transfers between devices: 1.7 us -> 0.01 us  [local(): lax.all_to_all(jnp.broadcast_to(norm[None], (peers, *norm.shape)), WIDTH,...]
  transfers between devices with their start and end apart: 1 -> 1, of which waited for: 1 -> 0; matrix products, arithmetic and copies ran while one was open for 4% -> 0% of each run, Pallas kernels for 0% -> 10%
where the time goes in v2:
time: 91.6 us; the launch traced here: 91 us
  blocking collectives  66.7 us (73%)
  Pallas kernels  11.1 us (12%)
  starting transfers between devices  7.17 us (8%)
  other arithmetic  3.99 us (4%)
  local copies, waits for them, and re-layouts  1.41 us (2%)
    all_gather x1, blocking collectives, local(): gathered = lax.all_gather(payload.astype(jnp.float16), 'fsdp', axis=0)  66.7 us
    pallas_call x1, Pallas kernels, local(): pl.pallas_call(functools.partial(merge, rows), out_shape=(*final, *scale)...  9.24 us
    all_to_all x1, starting transfers between devices, local(): lax.all_to_all(jnp.broadcast_to(norm[None], (peers, *norm.shape)), WIDTH,...  7.17 us
    convert_element_type x1, other arithmetic, local(): blocks = gathered.astype(jnp.bfloat16)  2.98 us
  transfers between devices with their start and end apart: 1, of which 0 were waited for; matrix products, arithmetic and copies ran while one was open for 0% of the time, Pallas kernels for 10%

profile of v2, /device:TPU:24, one launch (start us, length us, event | category | flops | bytes accessed | tf_op | source)
XLA Modules:
  0.0 91.0 jit_solution(15555211964918390608)
XLA Ops:
  0.6 1.8 %pack.1 = bf16[256,512]{1,0:T(8,128)(2,1)} custom-call(bf16[224,256]{1,0:T(8,128)(2,1)} %refs_0_.1, bf16[224,128]{1,0:T(8,128)(2,1)} %refs_1_.1, bf16[224,128]{1,0:T(8,128)(2,1)} %refs_2_.1, bf16[16,224]{1,0:T(8,128)(2,1)} %bitcast.17, bf16[16,224]{1,0:T(8,128)(2,1)} %bitcast.18, bf16[16,224]{1,0:T(8,128)(2,1)} %bitcast.19, f32[1,14]{1,0:T(1,128)} %bitcast.20, ...), custom_call_target="tpu_custom_call" | custom-call | tf_op jit(solution)/shard_map/pack/pallas_call | solution.py:204
  2.5 1.0 %convert_element_type.16 = f16[256,512]{1,0:T(8,128)(2,1)S(1)} convert(bf16[256,512]{1,0:T(8,128)(2,1)} %pack.1) | non-fusion elementwise | flops 131072 | bytes 524288 | tf_op jit(solution)/shard_map/convert_element_type | solution.py:216
  3.5 66.7 %all-gather.2 = f16[4096,512]{1,0:T(8,128)(2,1)S(1)} all-gather(f16[256,512]{1,0:T(8,128)(2,1)S(1)} %convert_element_type.16), channel_id=2, replica_groups=mesh['fsdp'=16,'width_0'=4,'width_1'=4,'trial'=2] {'fsdp'}, dimensions={0}, use_global_device_ids=true | all-gather | bytes 4456448 | tf_op jit(solution)/shard_map/all_gather | solution.py:216
  70.2 3.0 %convert_element_type.20.source = bf16[16,256,512]{2,1,0:T(8,128)(2,1)} convert(f16[16,256,512]{2,1,0:T(8,128)(2,1)S(1)} %bitcast.14) | non-fusion elementwise | flops 2097152 | bytes 8388608 | tf_op jit(solution)/shard_map/convert_element_type | solution.py:217
  73.2 0.6 broadcast_in_dim.2
  73.8 7.2 %all-to-all-start = ((bf16[16,16,14]{2,1,0:T(8,128)(2,1)}), bf16[16,16,14]{2,1,0:T(8,128)(2,1)S(1)}, u32[]{:S(2)}, u32[]{:S(2)}) async-start(bf16[16,16,14]{2,1,0:T(8,128)(2,1)} %broadcast_in_dim.2), calls=%async_computation | async-start | bytes 131072 | tf_op jit(solution)/shard_map/all_to_all | solution.py:221
  81.0 9.2 %merge.1 = (bf16[3584,256]{1,0:T(8,128)(2,1)}, bf16[3584,128]{1,0:T(8,128)(2,1)}, bf16[3584,128]{1,0:T(8,128)(2,1)}, f32[1,256]{1,0:T(1,128)}, f32[1,128]{1,0:T(1,128)}, /*index=5*/f32[1,128]{1,0:T(1,128)}) custom-call(bf16[16,256,512]{2,1,0:T(8,128)(2,1)} %convert_element_type.20.source, bf16[16,256]{1,0:T(8,128)(2,1)} %sq.1, bf16[16,128]{1,0:T(8,128)(2,1)} %sk.1, ...), custom_call_target="tpu_custom_call" | custom-call | flops 176160768 | bytes 12582912 | tf_op jit(solution)/shard_map/merge/pallas_call | solution.py:228
  90.2 0.0 all-to-all-done
  90.3 0.8 reshape.42
  (3 shorter events, 0.0 us)
Async XLA Ops:
  73.8 16.4 %all-to-all-start = ((bf16[16,16,14]{2,1,0:T(8,128)(2,1)}), bf16[16,16,14]{2,1,0:T(8,128)(2,1)S(1)}, u32[]{:S(2)}, u32[]{:S(2)}) async-start(bf16[16,16,14]{2,1,0:T(8,128)(2,1)} %broadcast_in_dim.2), calls=%async_computation | async-start | bytes 131072 | tf_op jit(solution)/shard_map/all_to_all | solution.py:221

commit v3 on v2

--- a/solution.py
+++ b/solution.py
@@ -20,6 +20,8 @@
 NORM_SCALE = 2.0**14
 
 ALL_VMEM = 60 * 1024 * 1024
+TOGETHER = 4
+CHUNK = 32
 
 
 def tier_of(largest):
@@ -119,27 +121,34 @@
         axis=0,
     ).astype(jnp.bfloat16)
 
-    def first(z, largest):
-        arrival(z).wait()
-        tier = blocks[z, rows + 24 : rows + 32, :].astype(jnp.float32)[0:1]
-        inverse = power(tier, -1)
-        left = blocks[z, rows : rows + 24, :half].astype(jnp.float32)
-        right = blocks[z, rows : rows + 24, half:].astype(jnp.float32)
-        low = jnp.concatenate([left[:16], right[:16], left[16:], right[16:]], axis=0)
-        low = low * power(low[:, rows : rows + 1], -1)
-        product = lax.dot_general(
-            low[:, :rows].astype(jnp.bfloat16),
-            high,
-            (((0,), (0,)), ((), ())),
-            preferred_element_type=jnp.float32,
-        )
-        merged = blocks[z, :rows, :].astype(jnp.float32) * inverse + product
-        result[z] = merged
-        return jnp.maximum(
-            largest, jnp.max(jnp.abs(merged).reshape(rows // 8, 8, columns), axis=0)
-        )
-
-    largest = lax.fori_loop(0, n, first, jnp.zeros((8, columns), jnp.float32))
+    def first(turn, largest):
+        these = [turn * TOGETHER + i for i in range(TOGETHER)]
+        inverses = []
+        for z in these:
+            arrival(z).wait()
+        for z in these:
+            tier = blocks[z, rows + 24 : rows + 32, :].astype(jnp.float32)[0:1]
+            inverses.append(power(tier, -1))
+            left = blocks[z, rows : rows + 24, :half].astype(jnp.float32)
+            right = blocks[z, rows : rows + 24, half:].astype(jnp.float32)
+            low = jnp.concatenate([left[:16], right[:16], left[16:], right[16:]], axis=0)
+            low = low * power(low[:, rows : rows + 1], -1)
+            result[z] = lax.dot_general(
+                low[:, :rows].astype(jnp.bfloat16),
+                high,
+                (((0,), (0,)), ((), ())),
+                preferred_element_type=jnp.float32,
+            )
+        for z, inverse in zip(these, inverses):
+            for r in range(0, rows, CHUNK):
+                part = slice(r, r + CHUNK)
+                merged = blocks[z, part, :].astype(jnp.float32) * inverse + result[z, part, :]
+                result[z, part, :] = merged
+                for i in range(0, CHUNK, 8):
+                    largest = jnp.maximum(largest, jnp.abs(merged[i : i + 8]))
+        return largest
+
+    largest = lax.fori_loop(0, n // TOGETHER, first, jnp.zeros((8, columns), jnp.float32))
     scale = jnp.max(largest, axis=0, keepdims=True)
     cq[...] = scale[:, :q]
     ck[...] = scale[:, q : q + kv]
@@ -154,10 +163,12 @@
         ]
 
     def second(z, carry):
-        final = (result[z] * inverse).astype(jnp.bfloat16)
-        oq[z] = final[:, :q]
-        ok[z] = final[:, q : q + kv]
-        ov[z] = final[:, q + kv :]
+        for r in range(0, rows, CHUNK):
+            part = slice(r, r + CHUNK)
+            final = (result[z, part, :] * inverse).astype(jnp.bfloat16)
+            oq[z, part, :] = final[:, :q]
+            ok[z, part, :] = final[:, q : q + kv]
+            ov[z, part, :] = final[:, q + kv :]
         for c in copies(z):
             c.start()
         return carry

time: 91.6 us -> 89 us (0.972)
  Pallas kernels: 11.1 us -> 8.44 us
    pallas_call x1, Pallas kernels: 9.24 us -> 6.63 us  [local(): pl.pallas_call(functools.partial(merge, rows), out_shape=(*final, *scale)...]
  transfers between devices with their start and end apart: 1 -> 1, of which waited for: 0 -> 0; matrix products, arithmetic and copies ran while one was open for 0% -> 0% of each run, Pallas kernels for 10% -> 7%
where the time goes in v3:
time: 89 us; the launch traced here: 88.4 us
  blocking collectives  66.7 us (75%)
  Pallas kernels  8.44 us (9%)
  starting transfers between devices  7.17 us (8%)
  other arithmetic  3.99 us (4%)
  local copies, waits for them, and re-layouts  1.41 us (2%)
    all_gather x1, blocking collectives, local(): gathered = lax.all_gather(payload.astype(jnp.float16), 'fsdp', axis=0)  66.7 us
    all_to_all x1, starting transfers between devices, local(): lax.all_to_all(jnp.broadcast_to(norm[None], (peers, *norm.shape)), WIDTH,...  7.17 us
    pallas_call x1, Pallas kernels, local(): pl.pallas_call(functools.partial(merge, rows), out_shape=(*final, *scale)...  6.63 us
    convert_element_type x1, other arithmetic, local(): blocks = gathered.astype(jnp.bfloat16)  2.98 us
    pallas_call x1, Pallas kernels, local(): pl.pallas_call(functools.partial(pack, rows), out_shape=jax.ShapeDtypeStr...  1.82 us
  transfers between devices with their start and end apart: 1, of which 0 were waited for; matrix products, arithmetic and copies ran while one was open for 0% of the time, Pallas kernels for 7%

profile of v3, /device:TPU:24, one launch (start us, length us, event | category | flops | bytes accessed | tf_op | source)
XLA Modules:
  0.0 88.4 jit_solution(274976556864331423)
XLA Ops:
  0.6 1.8 %pack.1 = bf16[256,512]{1,0:T(8,128)(2,1)} custom-call(bf16[224,256]{1,0:T(8,128)(2,1)} %refs_0_.1, bf16[224,128]{1,0:T(8,128)(2,1)} %refs_1_.1, bf16[224,128]{1,0:T(8,128)(2,1)} %refs_2_.1, bf16[16,224]{1,0:T(8,128)(2,1)} %bitcast.17, bf16[16,224]{1,0:T(8,128)(2,1)} %bitcast.18, bf16[16,224]{1,0:T(8,128)(2,1)} %bitcast.19, f32[1,14]{1,0:T(1,128)} %bitcast.20, ...), custom_call_target="tpu_custom_call" | custom-call | tf_op jit(solution)/shard_map/pack/pallas_call | solution.py:215
  2.5 1.0 %convert_element_type.16 = f16[256,512]{1,0:T(8,128)(2,1)S(1)} convert(bf16[256,512]{1,0:T(8,128)(2,1)} %pack.1) | non-fusion elementwise | flops 131072 | bytes 524288 | tf_op jit(solution)/shard_map/convert_element_type | solution.py:227
  3.5 66.7 %all-gather.2 = f16[4096,512]{1,0:T(8,128)(2,1)S(1)} all-gather(f16[256,512]{1,0:T(8,128)(2,1)S(1)} %convert_element_type.16), channel_id=2, replica_groups=mesh['fsdp'=16,'width_0'=4,'width_1'=4,'trial'=2] {'fsdp'}, dimensions={0}, use_global_device_ids=true | all-gather | bytes 4456448 | tf_op jit(solution)/shard_map/all_gather | solution.py:227
  70.2 3.0 %convert_element_type.20.source = bf16[16,256,512]{2,1,0:T(8,128)(2,1)} convert(f16[16,256,512]{2,1,0:T(8,128)(2,1)S(1)} %bitcast.14) | non-fusion elementwise | flops 2097152 | bytes 8388608 | tf_op jit(solution)/shard_map/convert_element_type | solution.py:228
  73.2 0.6 broadcast_in_dim.2
  73.8 7.2 %all-to-all-start = ((bf16[16,16,14]{2,1,0:T(8,128)(2,1)}), bf16[16,16,14]{2,1,0:T(8,128)(2,1)S(1)}, u32[]{:S(2)}, u32[]{:S(2)}) async-start(bf16[16,16,14]{2,1,0:T(8,128)(2,1)} %broadcast_in_dim.2), calls=%async_computation | async-start | bytes 131072 | tf_op jit(solution)/shard_map/all_to_all | solution.py:232
  81.0 6.6 %merge.1 = (bf16[3584,256]{1,0:T(8,128)(2,1)}, bf16[3584,128]{1,0:T(8,128)(2,1)}, bf16[3584,128]{1,0:T(8,128)(2,1)}, f32[1,256]{1,0:T(1,128)}, f32[1,128]{1,0:T(1,128)}, /*index=5*/f32[1,128]{1,0:T(1,128)}) custom-call(bf16[16,256,512]{2,1,0:T(8,128)(2,1)} %convert_element_type.20.source, bf16[16,256]{1,0:T(8,128)(2,1)} %sq.1, bf16[16,128]{1,0:T(8,128)(2,1)} %sk.1, ...), custom_call_target="tpu_custom_call" | custom-call | flops 176160768 | bytes 12582912 | tf_op jit(solution)/shard_map/merge/pallas_call | solution.py:239
  87.6 0.0 all-to-all-done
  87.7 0.8 reshape.42
  (3 shorter events, 0.0 us)
Async XLA Ops:
  73.8 13.8 %all-to-all-start = ((bf16[16,16,14]{2,1,0:T(8,128)(2,1)}), bf16[16,16,14]{2,1,0:T(8,128)(2,1)S(1)}, u32[]{:S(2)}, u32[]{:S(2)}) async-start(bf16[16,16,14]{2,1,0:T(8,128)(2,1)} %broadcast_in_dim.2), calls=%async_computation | async-start | bytes 131072 | tf_op jit(solution)/shard_map/all_to_all | solution.py:232

commit v4 on v3

--- a/solution.py
+++ b/solution.py
@@ -39,7 +39,7 @@
 
 
 def pack(rows, *refs):
-    sources, out, held, sems = refs[:8], refs[8], refs[9:17], refs[17]
+    sources, out, held, sems = refs[:6], refs[6], refs[7:13], refs[13]
     copies = [
         pltpu.make_async_copy(source, to, sems.at[i])
         for i, (source, to) in enumerate(zip(sources, held))
@@ -48,7 +48,7 @@
         c.start()
     for c in copies:
         c.wait()
-    wq, wk, wv, lq, lk, lv, train, step = held
+    wq, wk, wv, lq, lk, lv = held
     half = out.shape[1] // 2
     tiers = []
     at = 0
@@ -73,40 +73,13 @@
             row += rows
             out[row : row + b - a, column : column + rows] = low[a:b].astype(jnp.bfloat16)
             out[row : row + b - a, column + rows : column + half] = spare[a:b].astype(jnp.bfloat16)
-    norm = (train[...] + step[...]).astype(jnp.bfloat16).astype(jnp.float32) * NORM_SCALE
     index = lax.broadcasted_iota(jnp.int32, (8, out.shape[1]), 0)
     last = jnp.where(index == 0, jnp.broadcast_to(tier, index.shape), 0.0)
     out[rows + 24 : rows + 32, :] = last.astype(jnp.bfloat16)
-    n = norm.shape[1]
-    first = lax.broadcasted_iota(jnp.int32, (8, n), 0)
-    last = jnp.where(
-        first == 0, jnp.broadcast_to(tier[:, :n], first.shape), jnp.broadcast_to(norm, first.shape)
-    )
-    out[rows + 24 : rows + 32, :n] = last.astype(jnp.bfloat16)
-
-
-def merge(
-    rows, source, sq, sk, sv, fq, fk, fv, cq, ck, cv,
-    blocks, hq, hk, hv, result, oq, ok, ov, sems, arrived, ready,
-):
+
+
+def merge(rows, blocks, hq, hk, hv, fq, fk, fv, cq, ck, cv, result, oq, ok, ov, sems):
     n, _, columns = blocks.shape
-    highs = [
-        pltpu.make_async_copy(s, h, ready.at[i])
-        for i, (s, h) in enumerate(((sq, hq), (sk, hk), (sv, hv)))
-    ]
-    for c in highs:
-        c.start()
-
-    def arrival(z):
-        return pltpu.make_async_copy(source.at[z], blocks.at[z], arrived.at[z])
-
-    def fetch(z, carry):
-        arrival(z).start()
-        return carry
-
-    lax.fori_loop(0, n, fetch, 0)
-    for c in highs:
-        c.wait()
     half = columns // 2
     q, kv = hq.shape[1], hk.shape[1]
     rank = hq.shape[0]
@@ -124,8 +97,6 @@
     def first(turn, largest):
         these = [turn * TOGETHER + i for i in range(TOGETHER)]
         inverses = []
-        for z in these:
-            arrival(z).wait()
         for z in these:
             tier = blocks[z, rows + 24 : rows + 32, :].astype(jnp.float32)[0:1]
             inverses.append(power(tier, -1))
@@ -199,19 +170,14 @@
     rows, q = weight_query.shape
     kv = weight_key.shape[1]
     columns = q + 2 * kv
-    n = norm_train.shape[0]
     shards, peers = lax.axis_size("fsdp"), lax.axis_size(WIDTH)
 
-    sources = (
-        weight_query,
-        weight_key,
-        weight_value,
-        low_query.T,
-        low_key.T,
-        low_value.T,
-        norm_train.reshape(1, n),
-        norm_step.reshape(1, n),
+    norm = (norm_train + norm_step).astype(jnp.bfloat16)
+    norm = lax.all_to_all(
+        jnp.broadcast_to(norm[None], (peers, *norm.shape)), WIDTH, 0, 0, tiled=True
     )
+
+    sources = (weight_query, weight_key, weight_value, low_query.T, low_key.T, low_value.T)
     payload = pl.pallas_call(
         functools.partial(pack, rows),
         out_shape=jax.ShapeDtypeStruct((rows + 32, columns), jnp.bfloat16),
@@ -224,14 +190,11 @@
         compiler_params=pltpu.CompilerParams(vmem_limit_bytes=ALL_VMEM),
         name="pack",
     )(*sources)
-    gathered = lax.all_gather(payload.astype(jnp.float16), "fsdp", axis=0)
-    blocks = gathered.astype(jnp.bfloat16)
-
-    norm = gathered[:, rows + 25, :n].astype(jnp.float32) * (1.0 / NORM_SCALE)
-    norm, blocks = lax.optimization_barrier((norm.astype(jnp.bfloat16), blocks))
-    norm = lax.all_to_all(
-        jnp.broadcast_to(norm[None], (peers, *norm.shape)), WIDTH, 0, 0, tiled=True
-    )
+    norm = (norm.astype(jnp.float32) * NORM_SCALE).astype(jnp.float16).reshape(1, -1)
+    payload = lax.dynamic_update_slice(payload.astype(jnp.float16), norm, (rows + 25, 0))
+    blocks = lax.all_gather(payload, "fsdp", axis=0).astype(jnp.bfloat16)
+    serve_norm = blocks[:, rows + 25, : norm.shape[1]].astype(jnp.float32) * (1.0 / NORM_SCALE)
+    serve_norm = serve_norm.astype(jnp.bfloat16)
 
     vmem = pl.BlockSpec(memory_space=pltpu.VMEM)
     final = [jax.ShapeDtypeStruct((shards * rows, w), jnp.bfloat16) for w in (q, kv, kv)]
@@ -239,25 +202,21 @@
     out = pl.pallas_call(
         functools.partial(merge, rows),
         out_shape=(*final, *scale),
-        in_specs=[pl.BlockSpec(memory_space=pltpu.HBM)] * 4,
+        in_specs=[vmem] * 4,
         out_specs=(*[pl.BlockSpec(memory_space=pl.ANY)] * 3, *[vmem] * 3),
         scratch_shapes=[
-            pltpu.VMEM(blocks.shape, jnp.bfloat16),
-            *[pltpu.VMEM(h.shape, jnp.bfloat16) for h in (high_query, high_key, high_value)],
             pltpu.VMEM((shards, rows, columns), jnp.float32),
             *[pltpu.VMEM((shards, rows, w), jnp.bfloat16) for w in (q, kv, kv)],
             pltpu.SemaphoreType.DMA((3, shards)),
-            pltpu.SemaphoreType.DMA((shards,)),
-            pltpu.SemaphoreType.DMA((3,)),
         ],
-        compiler_params=pltpu.CompilerParams(vmem_limit_bytes=ALL_VMEM),
+        compiler_params=pltpu.CompilerParams(vmem_limit_bytes=24 << 20),
         cost_estimate=pl.CostEstimate(
             flops=2 * shards * rows * columns * 48, bytes_accessed=12 << 20, transcendentals=0
         ),
         name="merge",
     )(blocks, high_query, high_key, high_value)
-    serve_norm = norm.transpose(1, 0, 2).reshape(-1)
-    return (*out[:3], *(c.reshape(-1) for c in out[3:]), serve_norm)
+    serve_norm, out = lax.optimization_barrier((serve_norm, out))
+    return (*out[:3], *(c.reshape(-1) for c in out[3:]), serve_norm.reshape(-1))
 
 
 def solution(mesh):

time: 89 us -> 90.9 us (1.021)
  waiting for transfers between devices: 0.01 us -> 2.69 us
  starting transfers between devices: 7.17 us -> 8.9 us
  Pallas kernels: 8.44 us -> 7.05 us
  other arithmetic: 3.99 us -> 2.7 us
    all_to_all x1, waiting for transfers between devices: 0.01 us -> 2.69 us  [local(): lax.all_to_all(jnp.broadcast_to(norm[None], (peers, *norm.shape)), WIDTH,...]
    convert_element_type x3 -> x4, other arithmetic: 3.99 us -> 1.7 us  [the longest x1 0.96 us: local(): blocks = lax.all_gather(payload, 'fsdp', axis=0).astype(jnp.bfloat16)]
    all_to_all x1, starting transfers between devices: 7.17 us -> 8.9 us  [local(): lax.all_to_all(jnp.broadcast_to(norm[None], (peers, *norm.shape)), WIDTH,...]
    pallas_call x1, Pallas kernels: 6.63 us -> 5.25 us  [local(): pl.pallas_call(functools.partial(merge, rows), out_shape=(*final, *scale)...]
    all_gather x0 -> x1, other arithmetic: none -> 1 us  [local(): blocks = lax.all_gather(payload, 'fsdp', axis=0).astype(jnp.bfloat16)]
  transfers between devices with their start and end apart: 1 -> 1, of which waited for: 0 -> 1; matrix products, arithmetic and copies ran while one was open for 0% -> 1% of each run, Pallas kernels for 7% -> 2%
where the time goes in v4:
time: 90.9 us; the launch traced here: 89.8 us
  blocking collectives  66.1 us (73%)
  starting transfers between devices  8.9 us (10%)
  Pallas kernels  7.05 us (8%)
  other arithmetic  2.7 us (3%)
  waiting for transfers between devices  2.69 us (3%)
  local copies, waits for them, and re-layouts  1.65 us (2%)
    all_gather x1, blocking collectives, local(): blocks = lax.all_gather(payload, 'fsdp', axis=0).astype(jnp.bfloat16)  66.1 us
    all_to_all x1, starting transfers between devices, local(): lax.all_to_all(jnp.broadcast_to(norm[None], (peers, *norm.shape)), WIDTH,...  8.9 us
    pallas_call x1, Pallas kernels, local(): pl.pallas_call(functools.partial(merge, rows), out_shape=(*final, *scale)...  5.25 us
    all_to_all x1, waiting for transfers between devices, local(): lax.all_to_all(jnp.broadcast_to(norm[None], (peers, *norm.shape)), WIDTH,...  2.69 us
  transfers between devices with their start and end apart: 1, of which 1 were waited for; matrix products, arithmetic and copies ran while one was open for 1% of the time, Pallas kernels for 2%

profile of v4, /device:TPU:24, one launch (start us, length us, event | category | flops | bytes accessed | tf_op | source)
XLA Modules:
  0.0 89.8 jit_solution(2013747281800887637)
XLA Ops:
  0.6 0.7 add_convert_fusion
  1.3 0.6 broadcast_in_dim.2
  1.9 8.9 %all-to-all-start = ((bf16[16,1,14]{2,1,0:T(2,128)(2,1)}), bf16[16,1,14]{2,1,0:T(2,128)(2,1)S(1)}, u32[]{:S(2)}, u32[]{:S(2)}) async-start(bf16[16,1,14]{2,1,0:T(2,128)(2,1)} %broadcast_in_dim.2), calls=%async_computation | async-start | bytes 16384 | tf_op jit(solution)/shard_map/all_to_all | solution.py:176
  10.8 1.8 %pack.1 = bf16[256,512]{1,0:T(8,128)(2,1)} custom-call(bf16[224,256]{1,0:T(8,128)(2,1)} %refs_0_.1, bf16[224,128]{1,0:T(8,128)(2,1)} %refs_1_.1, bf16[224,128]{1,0:T(8,128)(2,1)} %refs_2_.1, bf16[16,224]{1,0:T(8,128)(2,1)} %bitcast.12, bf16[16,224]{1,0:T(8,128)(2,1)} %bitcast.13, bf16[16,224]{1,0:T(8,128)(2,1)} %bitcast.14), custom_call_target="tpu_custom_call" | custom-call | tf_op jit(solution)/shard_map/pack/pallas_call | solution.py:181
  12.6 1.0 %convert_bitcast_fusion = f16[1,256,512]{2,1,0:T(8,128)(2,1)S(1)} fusion(bf16[256,512]{1,0:T(8,128)(2,1)} %pack.1), kind=kLoop, calls=%fused_computation | loop fusion | flops 131072 | bytes 524288 | tf_op jit(solution)/shard_map/all_gather | solution.py:195
  13.6 2.7 %all-to-all-done = bf16[16,1,14]{2,1,0:T(2,128)(2,1)S(1)} async-done(((bf16[16,1,14]{2,1,0:T(2,128)(2,1)}), bf16[16,1,14]{2,1,0:T(2,128)(2,1)S(1)}, u32[]{:S(2)}, u32[]{:S(2)}) %all-to-all-start) | async-done | bytes 480 | tf_op jit(solution)/shard_map/all_to_all | solution.py:176
  16.4 0.1 convert_element_type.49
  16.5 0.2 dynamic_update_slice.4
  16.7 66.1 %all-gather.1 = f16[16,256,512]{2,1,0:T(8,128)(2,1)S(1)} all-gather(f16[1,256,512]{2,1,0:T(8,128)(2,1)S(1)} %dynamic_update_slice.4), channel_id=1, replica_groups=mesh['fsdp'=16,'width_0'=4,'width_1'=4,'trial'=2] {'fsdp'}, dimensions={0}, use_global_device_ids=true | all-gather | bytes 4456448 | tf_op jit(solution)/shard_map/all_gather | solution.py:195
  82.8 0.0 copy-start
  82.8 0.0 copy-start.1
  82.8 0.0 copy-start.2
  82.8 1.0 %convert_element_type.50.blocks = bf16[16,256,512]{2,1,0:T(8,128)(2,1)S(1)} convert(f16[16,256,512]{2,1,0:T(8,128)(2,1)S(1)} %all-gather.1) | non-fusion elementwise | flops 2097152 | bytes 8388608 | tf_op jit(solution)/shard_map/convert_element_type | solution.py:195
  83.8 0.0 copy-done
  83.8 0.0 copy-done.1
  83.8 0.0 copy-done.2
  83.8 5.3 %merge.1 = (bf16[3584,256]{1,0:T(8,128)(2,1)}, bf16[3584,128]{1,0:T(8,128)(2,1)}, bf16[3584,128]{1,0:T(8,128)(2,1)}, f32[1,256]{1,0:T(1,128)}, f32[1,128]{1,0:T(1,128)}, /*index=5*/f32[1,128]{1,0:T(1,128)}) custom-call(bf16[16,256,512]{2,1,0:T(8,128)(2,1)S(1)} %convert_element_type.50.blocks, bf16[16,256]{1,0:T(8,128)(2,1)S(1)} %copy-done, ...), custom_call_target="tpu_custom_call" | custom-call | flops 176160768 | bytes 12582912 | tf_op jit(solution)/shard_map/merge/pallas_call | solution.py:202
  89.1 0.7 reshape.63
  (3 shorter events, 0.1 us)
Async XLA Ops:
  1.9 14.4 %all-to-all-start = ((bf16[16,1,14]{2,1,0:T(2,128)(2,1)}), bf16[16,1,14]{2,1,0:T(2,128)(2,1)S(1)}, u32[]{:S(2)}, u32[]{:S(2)}) async-start(bf16[16,1,14]{2,1,0:T(2,128)(2,1)} %broadcast_in_dim.2), calls=%async_computation | async-start | bytes 16384 | tf_op jit(solution)/shard_map/all_to_all | solution.py:176
  82.8 1.0 %copy-start = (bf16[16,256]{1,0:T(8,128)(2,1)S(1)}, bf16[16,256]{1,0:T(8,128)(2,1)}, u32[]{:S(2)}) copy-start(bf16[16,256]{1,0:T(8,128)(2,1)} %hq.1) | copy-start | bytes 24580
  82.8 1.0 %copy-start.1 = (bf16[16,128]{1,0:T(8,128)(2,1)S(1)}, bf16[16,128]{1,0:T(8,128)(2,1)}, u32[]{:S(2)}) copy-start(bf16[16,128]{1,0:T(8,128)(2,1)} %hk.1) | copy-start | bytes 12292
  82.8 1.0 %copy-start.2 = (bf16[16,128]{1,0:T(8,128)(2,1)S(1)}, bf16[16,128]{1,0:T(8,128)(2,1)}, u32[]{:S(2)}) copy-start(bf16[16,128]{1,0:T(8,128)(2,1)} %hv.1) | copy-start | bytes 12292

commit v5 on v3

--- a/solution.py
+++ b/solution.py
@@ -85,28 +85,8 @@
     out[rows + 24 : rows + 32, :n] = last.astype(jnp.bfloat16)
 
 
-def merge(
-    rows, source, sq, sk, sv, fq, fk, fv, cq, ck, cv,
-    blocks, hq, hk, hv, result, oq, ok, ov, sems, arrived, ready,
-):
+def merge(rows, blocks, hq, hk, hv, fq, fk, fv, cq, ck, cv, result, oq, ok, ov, sems):
     n, _, columns = blocks.shape
-    highs = [
-        pltpu.make_async_copy(s, h, ready.at[i])
-        for i, (s, h) in enumerate(((sq, hq), (sk, hk), (sv, hv)))
-    ]
-    for c in highs:
-        c.start()
-
-    def arrival(z):
-        return pltpu.make_async_copy(source.at[z], blocks.at[z], arrived.at[z])
-
-    def fetch(z, carry):
-        arrival(z).start()
-        return carry
-
-    lax.fori_loop(0, n, fetch, 0)
-    for c in highs:
-        c.wait()
     half = columns // 2
     q, kv = hq.shape[1], hk.shape[1]
     rank = hq.shape[0]
@@ -124,8 +104,6 @@
     def first(turn, largest):
         these = [turn * TOGETHER + i for i in range(TOGETHER)]
         inverses = []
-        for z in these:
-            arrival(z).wait()
         for z in these:
             tier = blocks[z, rows + 24 : rows + 32, :].astype(jnp.float32)[0:1]
             inverses.append(power(tier, -1))
@@ -225,13 +203,13 @@
         name="pack",
     )(*sources)
     gathered = lax.all_gather(payload.astype(jnp.float16), "fsdp", axis=0)
-    blocks = gathered.astype(jnp.bfloat16)
 
     norm = gathered[:, rows + 25, :n].astype(jnp.float32) * (1.0 / NORM_SCALE)
-    norm, blocks = lax.optimization_barrier((norm.astype(jnp.bfloat16), blocks))
+    norm = norm.astype(jnp.bfloat16)
     norm = lax.all_to_all(
         jnp.broadcast_to(norm[None], (peers, *norm.shape)), WIDTH, 0, 0, tiled=True
     )
+    blocks = gathered.astype(jnp.bfloat16)
 
     vmem = pl.BlockSpec(memory_space=pltpu.VMEM)
     final = [jax.ShapeDtypeStruct((shards * rows, w), jnp.bfloat16) for w in (q, kv, kv)]
@@ -239,18 +217,14 @@
     out = pl.pallas_call(
         functools.partial(merge, rows),
         out_shape=(*final, *scale),
-        in_specs=[pl.BlockSpec(memory_space=pltpu.HBM)] * 4,
+        in_specs=[vmem] * 4,
         out_specs=(*[pl.BlockSpec(memory_space=pl.ANY)] * 3, *[vmem] * 3),
         scratch_shapes=[
-            pltpu.VMEM(blocks.shape, jnp.bfloat16),
-            *[pltpu.VMEM(h.shape, jnp.bfloat16) for h in (high_query, high_key, high_value)],
             pltpu.VMEM((shards, rows, columns), jnp.float32),
             *[pltpu.VMEM((shards, rows, w), jnp.bfloat16) for w in (q, kv, kv)],
             pltpu.SemaphoreType.DMA((3, shards)),
-            pltpu.SemaphoreType.DMA((shards,)),
-            pltpu.SemaphoreType.DMA((3,)),
         ],
-        compiler_params=pltpu.CompilerParams(vmem_limit_bytes=ALL_VMEM),
+        compiler_params=pltpu.CompilerParams(vmem_limit_bytes=24 << 20),
         cost_estimate=pl.CostEstimate(
             flops=2 * shards * rows * columns * 48, bytes_accessed=12 << 20, transcendentals=0
         ),

time: 89 us -> 89.7 us (level)
  local copies, waits for them, and re-layouts: 1.41 us -> 3.37 us
  Pallas kernels: 8.44 us -> 7.07 us
    unnamed x1 -> x9, local copies, waits for them, and re-layouts: 0.01 us -> 1.96 us
    pallas_call x1, Pallas kernels: 6.63 us -> 5.25 us  [local(): pl.pallas_call(functools.partial(merge, rows), out_shape=(*final, *scale)...]
  transfers between devices with their start and end apart: 1 -> 1, of which waited for: 0 -> 0; matrix products, arithmetic and copies ran while one was open for 0% -> 3% of each run, Pallas kernels for 7% -> 6%
where the time goes in v5:
time: 89.7 us; the launch traced here: 89.1 us
  blocking collectives  66.7 us (74%)
  starting transfers between devices  7.17 us (8%)
  Pallas kernels  7.07 us (8%)
  other arithmetic  4.05 us (5%)
  local copies, waits for them, and re-layouts  3.37 us (4%)
    all_gather x1, blocking collectives, local(): gathered = lax.all_gather(payload.astype(jnp.float16), 'fsdp', axis=0)  66.7 us
    all_to_all x1, starting transfers between devices, local(): lax.all_to_all(jnp.broadcast_to(norm[None], (peers, *norm.shape)), WIDTH,...  7.17 us
    pallas_call x1, Pallas kernels, local(): pl.pallas_call(functools.partial(merge, rows), out_shape=(*final, *scale)...  5.25 us
    convert_element_type x1, other arithmetic, local(): blocks = gathered.astype(jnp.bfloat16)  3.04 us
    unnamed x9, local copies, waits for them, and re-layouts  1.96 us
    pallas_call x1, Pallas kernels, local(): pl.pallas_call(functools.partial(pack, rows), out_shape=jax.ShapeDtypeStr...  1.82 us
  transfers between devices with their start and end apart: 1, of which 0 were waited for; matrix products, arithmetic and copies ran while one was open for 3% of the time, Pallas kernels for 6%

profile of v5, /device:TPU:24, one launch (start us, length us, event | category | flops | bytes accessed | tf_op | source)
XLA Modules:
  0.0 89.1 jit_solution(15163057811517791090)
XLA Ops:
  0.6 1.8 %pack.1 = bf16[256,512]{1,0:T(8,128)(2,1)} custom-call(bf16[224,256]{1,0:T(8,128)(2,1)} %refs_0_.1, bf16[224,128]{1,0:T(8,128)(2,1)} %refs_1_.1, bf16[224,128]{1,0:T(8,128)(2,1)} %refs_2_.1, bf16[16,224]{1,0:T(8,128)(2,1)} %bitcast.17, bf16[16,224]{1,0:T(8,128)(2,1)} %bitcast.18, bf16[16,224]{1,0:T(8,128)(2,1)} %bitcast.19, f32[1,14]{1,0:T(1,128)} %bitcast.20, ...), custom_call_target="tpu_custom_call" | custom-call | tf_op jit(solution)/shard_map/pack/pallas_call | solution.py:193
  2.5 1.0 %convert_element_type.24 = f16[256,512]{1,0:T(8,128)(2,1)S(1)} convert(bf16[256,512]{1,0:T(8,128)(2,1)} %pack.1) | non-fusion elementwise | flops 131072 | bytes 524288 | tf_op jit(solution)/shard_map/convert_element_type | solution.py:205
  3.5 66.7 %all-gather.2 = f16[4096,512]{1,0:T(8,128)(2,1)S(1)} all-gather(f16[256,512]{1,0:T(8,128)(2,1)S(1)} %convert_element_type.24), channel_id=2, replica_groups=mesh['fsdp'=16,'width_0'=4,'width_1'=4,'trial'=2] {'fsdp'}, dimensions={0}, use_global_device_ids=true | all-gather | bytes 4456448 | tf_op jit(solution)/shard_map/all_gather | solution.py:205
  70.2 0.0 copy-start.3
  70.2 1.9 %copy-done.3 = f16[4096,512]{1,0:T(8,128)(2,1)} copy-done((f16[4096,512]{1,0:T(8,128)(2,1)}, f16[4096,512]{1,0:T(8,128)(2,1)S(1)}, u32[]{:S(2)}) %copy-start.3) | copy-done | bytes 4194328
  72.2 0.6 broadcast_in_dim.2
  72.8 7.2 %all-to-all-start = ((bf16[16,16,14]{2,1,0:T(8,128)(2,1)}), bf16[16,16,14]{2,1,0:T(8,128)(2,1)S(1)}, u32[]{:S(2)}, u32[]{:S(2)}) async-start(bf16[16,16,14]{2,1,0:T(8,128)(2,1)} %broadcast_in_dim.2), calls=%async_computation | async-start | bytes 131072 | tf_op jit(solution)/shard_map/all_to_all | solution.py:209
  80.0 0.0 copy-start
  80.0 0.0 copy-start.1
  80.0 0.0 copy-start.2
  80.0 3.0 %convert_element_type.25.blocks = bf16[16,256,512]{2,1,0:T(8,128)(2,1)S(1)} convert(f16[16,256,512]{2,1,0:T(8,128)(2,1)} %bitcast.14) | non-fusion elementwise | flops 2097152 | bytes 8388608 | tf_op jit(solution)/shard_map/convert_element_type | solution.py:212
  83.0 0.0 copy-done
  83.1 0.0 copy-done.1
  83.1 0.0 copy-done.2
  83.1 5.3 %merge.1 = (bf16[3584,256]{1,0:T(8,128)(2,1)}, bf16[3584,128]{1,0:T(8,128)(2,1)}, bf16[3584,128]{1,0:T(8,128)(2,1)}, f32[1,256]{1,0:T(1,128)}, f32[1,128]{1,0:T(1,128)}, /*index=5*/f32[1,128]{1,0:T(1,128)}) custom-call(bf16[16,256,512]{2,1,0:T(8,128)(2,1)S(1)} %convert_element_type.25.blocks, bf16[16,256]{1,0:T(8,128)(2,1)S(1)} %copy-done, ...), custom_call_target="tpu_custom_call" | custom-call | flops 176160768 | bytes 12582912 | tf_op jit(solution)/shard_map/merge/pallas_call | solution.py:217
  88.3 0.0 all-to-all-done
  88.4 0.8 reshape.48
  (3 shorter events, 0.0 us)
Async XLA Ops:
  70.2 1.9 %copy-start.3 = (f16[4096,512]{1,0:T(8,128)(2,1)}, f16[4096,512]{1,0:T(8,128)(2,1)S(1)}, u32[]{:S(2)}) copy-start(f16[4096,512]{1,0:T(8,128)(2,1)S(1)} %all-gather.2) | copy-start | bytes 12582916
  72.8 15.5 %all-to-all-start = ((bf16[16,16,14]{2,1,0:T(8,128)(2,1)}), bf16[16,16,14]{2,1,0:T(8,128)(2,1)S(1)}, u32[]{:S(2)}, u32[]{:S(2)}) async-start(bf16[16,16,14]{2,1,0:T(8,128)(2,1)} %broadcast_in_dim.2), calls=%async_computation | async-start | bytes 131072 | tf_op jit(solution)/shard_map/all_to_all | solution.py:209
  80.0 3.1 %copy-start = (bf16[16,256]{1,0:T(8,128)(2,1)S(1)}, bf16[16,256]{1,0:T(8,128)(2,1)}, u32[]{:S(2)}) copy-start(bf16[16,256]{1,0:T(8,128)(2,1)} %hq.1) | copy-start | bytes 24580
  80.0 3.1 %copy-start.1 = (bf16[16,128]{1,0:T(8,128)(2,1)S(1)}, bf16[16,128]{1,0:T(8,128)(2,1)}, u32[]{:S(2)}) copy-start(bf16[16,128]{1,0:T(8,128)(2,1)} %hk.1) | copy-start | bytes 12292
  80.0 3.1 %copy-start.2 = (bf16[16,128]{1,0:T(8,128)(2,1)S(1)}, bf16[16,128]{1,0:T(8,128)(2,1)}, u32[]{:S(2)}) copy-start(bf16[16,128]{1,0:T(8,128)(2,1)} %hv.1) | copy-start | bytes 12292

commit v6 on v5

--- a/solution.py
+++ b/solution.py
@@ -21,6 +21,7 @@
 
 ALL_VMEM = 60 * 1024 * 1024
 TOGETHER = 4
+STAY = 12
 CHUNK = 32
 
 
@@ -36,6 +37,10 @@
     for t in range(TIERS - 1):
         p = p * jnp.where(k > t, 2.0 ** (sign * STEP), 1.0)
     return p
+
+
+def behind(shape, axis, rows):
+    return lax.broadcasted_iota(jnp.int32, shape, axis) - rows
 
 
 def pack(rows, *refs):
@@ -49,7 +54,9 @@
     for c in copies:
         c.wait()
     wq, wk, wv, lq, lk, lv, train, step = held
-    half = out.shape[1] // 2
+    columns = out.shape[1]
+    half = columns // 2
+    spare = half - rows
     tiers = []
     at = 0
     for w in (wq, wk, wv):
@@ -60,36 +67,66 @@
         tiers.append(tier)
         at += width
     tier = jnp.concatenate(tiers, axis=1)
-    for l, places in (
-        (lq, ((0, 16, 0, 0),)),
-        (lk, ((0, 16, 0, half),)),
-        (lv, ((0, 8, 16, 0), (8, 16, 16, half))),
-    ):
+
+    lows, low_tiers = [], []
+    for l in (lq, lk, lv):
         low = l[...].astype(jnp.float32)
         low_tier = tier_of(jnp.max(jnp.abs(low), axis=1, keepdims=True))
-        low = low * power(low_tier, 1)
-        spare = jnp.broadcast_to(low_tier, (low.shape[0], half - rows))
-        for a, b, row, column in places:
-            row += rows
-            out[row : row + b - a, column : column + rows] = low[a:b].astype(jnp.bfloat16)
-            out[row : row + b - a, column + rows : column + half] = spare[a:b].astype(jnp.bfloat16)
+        lows.append(low * power(low_tier, 1))
+        low_tiers.append(low_tier)
+    for left, right, row in (
+        ((0, 0, 16), (1, 0, 16), rows),
+        ((2, 0, 8), (2, 8, 16), rows + 16),
+    ):
+        (i, a, b), (j, c, d) = left, right
+        to = slice(row, row + b - a)
+        out[to, :rows] = lows[i][a:b].astype(jnp.bfloat16)
+        out[to, half : half + rows] = lows[j][c:d].astype(jnp.bfloat16)
+        shape = (b - a, half)
+        both = jnp.where(
+            behind(shape, 1, rows) < spare // 2,
+            jnp.broadcast_to(low_tiers[i][a:b], shape),
+            jnp.broadcast_to(low_tiers[j][c:d], shape),
+        )
+        out[to, half + rows :] = both[:, rows:].astype(jnp.bfloat16)
+
+    shape = (16, columns)
+    own = behind(shape, 1, 0) // spare == behind(shape, 0, 0)
+    spread = jnp.where(own, jnp.broadcast_to(tier, shape), 0.0).astype(jnp.bfloat16)
+    shape = (columns, half)
+    pick = behind(shape, 1, rows) == behind(shape, 0, 0) % spare
+    moved = jnp.dot(
+        spread, jnp.where(pick, 1.0, 0.0).astype(jnp.bfloat16), preferred_element_type=jnp.float32
+    )
+    out[rows : rows + 16, rows:half] = moved[:, rows:].astype(jnp.bfloat16)
     norm = (train[...] + step[...]).astype(jnp.bfloat16).astype(jnp.float32) * NORM_SCALE
-    index = lax.broadcasted_iota(jnp.int32, (8, out.shape[1]), 0)
-    last = jnp.where(index == 0, jnp.broadcast_to(tier, index.shape), 0.0)
-    out[rows + 24 : rows + 32, :] = last.astype(jnp.bfloat16)
     n = norm.shape[1]
-    first = lax.broadcasted_iota(jnp.int32, (8, n), 0)
-    last = jnp.where(
-        first == 0, jnp.broadcast_to(tier[:, :n], first.shape), jnp.broadcast_to(norm, first.shape)
-    )
-    out[rows + 24 : rows + 32, :n] = last.astype(jnp.bfloat16)
-
-
-def merge(rows, blocks, hq, hk, hv, fq, fk, fv, cq, ck, cv, result, oq, ok, ov, sems):
-    n, _, columns = blocks.shape
+    norm = jnp.broadcast_to(norm, (8, n)).astype(jnp.bfloat16)
+    shape = (n, half)
+    pick = behind(shape, 1, rows) == behind(shape, 0, 0)
+    moved = jnp.dot(
+        norm, jnp.where(pick, 1.0, 0.0).astype(jnp.bfloat16), preferred_element_type=jnp.float32
+    )
+    out[rows + 16 : rows + 24, rows:half] = moved[:, rows:].astype(jnp.bfloat16)
+
+
+def merge(
+    rows, stayed, left_out, hq, hk, hv, fq, fk, fv, cq, ck, cv,
+    back, result, oq, ok, ov, sems, arrived,
+):
+    columns = stayed.shape[2]
+    n = stayed.shape[0] + back.shape[0]
+    arrival = pltpu.make_async_copy(left_out, back, arrived)
+    arrival.start()
     half = columns // 2
+    spare = half - rows
     q, kv = hq.shape[1], hk.shape[1]
     rank = hq.shape[0]
+    shape = (half, columns)
+    pick = behind(shape, 0, rows) == behind(shape, 1, 0) % spare
+    pick = jnp.where(pick, 1.0, 0.0).astype(jnp.bfloat16)
+    shape = (16, columns)
+    own = behind(shape, 1, 0) // spare == behind(shape, 0, 0)
     high_q, high_k, high_v = (mix_rate * h[...].astype(jnp.float32) for h in (hq, hk, hv))
     none_q, none = jnp.zeros((rank, q), jnp.float32), jnp.zeros((rank, kv), jnp.float32)
     high = jnp.concatenate(
@@ -101,32 +138,46 @@
         axis=0,
     ).astype(jnp.bfloat16)
 
-    def first(turn, largest):
-        these = [turn * TOGETHER + i for i in range(TOGETHER)]
+    def turn(blocks, begin, to, largest):
         inverses = []
-        for z in these:
-            tier = blocks[z, rows + 24 : rows + 32, :].astype(jnp.float32)[0:1]
+        for i in range(TOGETHER):
+            left = blocks[begin + i, rows : rows + 24, :half].astype(jnp.float32)
+            right = blocks[begin + i, rows : rows + 24, half:].astype(jnp.float32)
+            tier = jnp.dot(
+                left[:16].astype(jnp.bfloat16), pick, preferred_element_type=jnp.float32
+            )
+            tier = jnp.sum(jnp.where(own, tier, 0.0), axis=0, keepdims=True)
             inverses.append(power(tier, -1))
-            left = blocks[z, rows : rows + 24, :half].astype(jnp.float32)
-            right = blocks[z, rows : rows + 24, half:].astype(jnp.float32)
+            middle = rows + spare // 2
+            left = left * power(right[:, rows : rows + 1], -1)
+            right = right * power(right[:, middle : middle + 1], -1)
             low = jnp.concatenate([left[:16], right[:16], left[16:], right[16:]], axis=0)
-            low = low * power(low[:, rows : rows + 1], -1)
-            result[z] = lax.dot_general(
+            result[to + i] = lax.dot_general(
                 low[:, :rows].astype(jnp.bfloat16),
                 high,
                 (((0,), (0,)), ((), ())),
                 preferred_element_type=jnp.float32,
             )
-        for z, inverse in zip(these, inverses):
+        for i, inverse in enumerate(inverses):
             for r in range(0, rows, CHUNK):
                 part = slice(r, r + CHUNK)
-                merged = blocks[z, part, :].astype(jnp.float32) * inverse + result[z, part, :]
-                result[z, part, :] = merged
-                for i in range(0, CHUNK, 8):
-                    largest = jnp.maximum(largest, jnp.abs(merged[i : i + 8]))
+                block = blocks[begin + i, part, :].astype(jnp.float32)
+                merged = block * inverse + result[to + i, part, :]
+                result[to + i, part, :] = merged
+                for j in range(0, CHUNK, 8):
+                    largest = jnp.maximum(largest, jnp.abs(merged[j : j + 8]))
         return largest
 
-    largest = lax.fori_loop(0, n // TOGETHER, first, jnp.zeros((8, columns), jnp.float32))
+    def first(t, largest):
+        return turn(stayed, t * TOGETHER, t * TOGETHER, largest)
+
+    kept = stayed.shape[0]
+    largest = lax.fori_loop(
+        0, kept // TOGETHER, first, jnp.zeros((8, columns), jnp.float32)
+    )
+    arrival.wait()
+    for t in range(0, n - kept, TOGETHER):
+        largest = turn(back, t, kept + t, largest)
     scale = jnp.max(largest, axis=0, keepdims=True)
     cq[...] = scale[:, :q]
     ck[...] = scale[:, q : q + kv]
@@ -192,7 +243,7 @@
     )
     payload = pl.pallas_call(
         functools.partial(pack, rows),
-        out_shape=jax.ShapeDtypeStruct((rows + 32, columns), jnp.bfloat16),
+        out_shape=jax.ShapeDtypeStruct((rows + 24, columns), jnp.bfloat16),
         in_specs=[pl.BlockSpec(memory_space=pltpu.HBM)] * len(sources),
         out_specs=pl.BlockSpec(memory_space=pltpu.VMEM),
         scratch_shapes=[
@@ -204,12 +255,17 @@
     )(*sources)
     gathered = lax.all_gather(payload.astype(jnp.float16), "fsdp", axis=0)
 
-    norm = gathered[:, rows + 25, :n].astype(jnp.float32) * (1.0 / NORM_SCALE)
-    norm = norm.astype(jnp.bfloat16)
+    norm = gathered[:, rows + 16, rows : rows + n].astype(jnp.float32) * (1.0 / NORM_SCALE)
+    norm, stayed, left_out = lax.optimization_barrier(
+        (
+            norm.astype(jnp.bfloat16),
+            gathered[:STAY].astype(jnp.bfloat16),
+            gathered[STAY:].astype(jnp.bfloat16),
+        )
+    )
     norm = lax.all_to_all(
         jnp.broadcast_to(norm[None], (peers, *norm.shape)), WIDTH, 0, 0, tiled=True
     )
-    blocks = gathered.astype(jnp.bfloat16)
 
     vmem = pl.BlockSpec(memory_space=pltpu.VMEM)
     final = [jax.ShapeDtypeStruct((shards * rows, w), jnp.bfloat16) for w in (q, kv, kv)]
@@ -217,19 +273,21 @@
     out = pl.pallas_call(
         functools.partial(merge, rows),
         out_shape=(*final, *scale),
-        in_specs=[vmem] * 4,
+        in_specs=[vmem, pl.BlockSpec(memory_space=pltpu.HBM), vmem, vmem, vmem],
         out_specs=(*[pl.BlockSpec(memory_space=pl.ANY)] * 3, *[vmem] * 3),
         scratch_shapes=[
+            pltpu.VMEM(left_out.shape, jnp.bfloat16),
             pltpu.VMEM((shards, rows, columns), jnp.float32),
             *[pltpu.VMEM((shards, rows, w), jnp.bfloat16) for w in (q, kv, kv)],
             pltpu.SemaphoreType.DMA((3, shards)),
+            pltpu.SemaphoreType.DMA,
         ],
         compiler_params=pltpu.CompilerParams(vmem_limit_bytes=24 << 20),
         cost_estimate=pl.CostEstimate(
             flops=2 * shards * rows * columns * 48, bytes_accessed=12 << 20, transcendentals=0
         ),
         name="merge",
-    )(blocks, high_query, high_key, high_value)
+    )(stayed, left_out, high_query, high_key, high_value)
     serve_norm = norm.transpose(1, 0, 2).reshape(-1)
     return (*out[:3], *(c.reshape(-1) for c in out[3:]), serve_norm)
 

time: 89.7 us -> 87.1 us (0.971)
  other arithmetic: 4.05 us -> 2.6 us
  blocking collectives: 66.7 us -> 65.7 us
    convert_element_type x2 -> x3, other arithmetic: 3.06 us -> 1.61 us  [the longest x1 1.11 us: local(): gathered[STAY:].astype(jnp.bfloat16)]
    all_gather x1, blocking collectives: 66.7 us -> 65.7 us  [local(): gathered = lax.all_gather(payload.astype(jnp.float16), 'fsdp', axis=0)]
    unnamed x9 -> x8, local copies, waits for them, and re-layouts: 1.96 us -> 1.22 us
  transfers between devices with their start and end apart: 1 -> 1, of which waited for: 0 -> 0; matrix products, arithmetic and copies ran while one was open for 3% -> 0% of each run, Pallas kernels for 6% -> 7%
where the time goes in v6:
time: 87.1 us; the launch traced here: 86.5 us
  blocking collectives  65.7 us (75%)
  Pallas kernels  7.63 us (9%)
  starting transfers between devices  7.17 us (8%)
  local copies, waits for them, and re-layouts  2.72 us (3%)
  other arithmetic  2.6 us (3%)
    all_gather x1, blocking collectives, local(): gathered = lax.all_gather(payload.astype(jnp.float16), 'fsdp', axis=0)  65.7 us
    all_to_all x1, starting transfers between devices, local(): lax.all_to_all(jnp.broadcast_to(norm[None], (peers, *norm.shape)), WIDTH,...  7.17 us
    pallas_call x1, Pallas kernels, local(): pl.pallas_call(functools.partial(merge, rows), out_shape=(*final, *scale)...  5.72 us
    pallas_call x1, Pallas kernels, local(): pl.pallas_call(functools.partial(pack, rows), out_shape=jax.ShapeDtypeStr...  1.9 us
  transfers between devices with their start and end apart: 1, of which 0 were waited for; matrix products, arithmetic and copies ran while one was open for 0% of the time, Pallas kernels for 7%

profile of v6, /device:TPU:24, one launch (start us, length us, event | category | flops | bytes accessed | tf_op | source)
XLA Modules:
  0.0 86.5 jit_solution(4978684656766036976)
XLA Ops:
  0.6 1.9 %pack.1 = bf16[248,512]{1,0:T(8,128)(2,1)} custom-call(bf16[224,256]{1,0:T(8,128)(2,1)} %refs_0_.1, bf16[224,128]{1,0:T(8,128)(2,1)} %refs_1_.1, bf16[224,128]{1,0:T(8,128)(2,1)} %refs_2_.1, bf16[16,224]{1,0:T(8,128)(2,1)} %bitcast.18, bf16[16,224]{1,0:T(8,128)(2,1)} %bitcast.19, bf16[16,224]{1,0:T(8,128)(2,1)} %bitcast.20, f32[1,14]{1,0:T(1,128)} %bitcast.21, ...), custom_call_target="tpu_custom_call" | custom-call | tf_op jit(solution)/shard_map/pack/pallas_call | solution.py:244
  2.5 1.0 %convert_element_type.19 = f16[248,512]{1,0:T(8,128)(2,1)S(1)} convert(bf16[248,512]{1,0:T(8,128)(2,1)} %pack.1) | non-fusion elementwise | flops 126976 | bytes 507904 | tf_op jit(solution)/shard_map/convert_element_type | solution.py:256
  3.5 65.7 %all-gather.2 = f16[3968,512]{1,0:T(8,128)(2,1)S(1)} all-gather(f16[248,512]{1,0:T(8,128)(2,1)S(1)} %convert_element_type.19), channel_id=2, replica_groups=mesh['fsdp'=16,'width_0'=4,'width_1'=4,'trial'=2] {'fsdp'}, dimensions={0}, use_global_device_ids=true | all-gather | bytes 4317184 | tf_op jit(solution)/shard_map/all_gather | solution.py:256
  69.2 1.1 %slice_convert_fusion.1 = bf16[992,512]{1,0:T(8,128)(2,1)} fusion(f16[3968,512]{1,0:T(8,128)(2,1)S(1)} %all-gather.2), kind=kLoop, calls=%fused_computation.1 | loop fusion | flops 507904 | bytes 2031616 | tf_op jit(solution)/shard_map/convert_element_type | solution.py:263
  70.3 0.0 copy-start.1
  70.3 0.0 copy-start.2
  70.3 0.0 copy-start.3
  70.3 0.5 slice_convert_fusion
  70.8 0.1 slice.14
  70.9 0.6 broadcast_in_dim.2
  71.6 7.2 %all-to-all-start = ((bf16[16,16,14]{2,1,0:T(8,128)(2,1)}), bf16[16,16,14]{2,1,0:T(8,128)(2,1)S(1)}, u32[]{:S(2)}, u32[]{:S(2)}) async-start(bf16[16,16,14]{2,1,0:T(8,128)(2,1)} %broadcast_in_dim.2), calls=%async_computation | async-start | bytes 131072 | tf_op jit(solution)/shard_map/all_to_all | solution.py:266
  78.8 0.0 copy-done.1
  78.8 0.0 copy-done.2
  78.8 0.0 copy-done.3
  78.8 0.0 copy-start
  78.8 1.2 %copy-done = bf16[992,512]{1,0:T(8,128)(2,1)S(1)} copy-done((bf16[992,512]{1,0:T(8,128)(2,1)S(1)}, bf16[992,512]{1,0:T(8,128)(2,1)}, u32[]{:S(2)}) %copy-start) | copy-done | bytes 1015832
  80.0 5.7 %merge.1 = (bf16[3584,256]{1,0:T(8,128)(2,1)}, bf16[3584,128]{1,0:T(8,128)(2,1)}, bf16[3584,128]{1,0:T(8,128)(2,1)}, f32[1,256]{1,0:T(1,128)}, f32[1,128]{1,0:T(1,128)}, /*index=5*/f32[1,128]{1,0:T(1,128)}) custom-call(bf16[12,248,512]{2,1,0:T(8,128)(2,1)S(1)} %bitcast.14, bf16[4,248,512]{2,1,0:T(8,128)(2,1)S(1)} %bitcast.15, bf16[16,256]{1,0:T(8,128)(2,1)S(1)} %copy-done.1, ...), custom_call_target="tpu_custom_call" | custom-call | flops 176160768 | bytes 12582912 | tf_op jit(solution)/shard_map/merge/pallas_call | solution.py:273
  85.7 0.0 all-to-all-done
  85.8 0.8 reshape.42
  (2 shorter events, 0.0 us)
Async XLA Ops:
  70.3 8.4 %copy-start.1 = (bf16[16,256]{1,0:T(8,128)(2,1)S(1)}, bf16[16,256]{1,0:T(8,128)(2,1)}, u32[]{:S(2)}) copy-start(bf16[16,256]{1,0:T(8,128)(2,1)} %hq.1) | copy-start | bytes 24580
  70.3 8.4 %copy-start.2 = (bf16[16,128]{1,0:T(8,128)(2,1)S(1)}, bf16[16,128]{1,0:T(8,128)(2,1)}, u32[]{:S(2)}) copy-start(bf16[16,128]{1,0:T(8,128)(2,1)} %hk.1) | copy-start | bytes 12292
  70.3 8.4 %copy-start.3 = (bf16[16,128]{1,0:T(8,128)(2,1)S(1)}, bf16[16,128]{1,0:T(8,128)(2,1)}, u32[]{:S(2)}) copy-start(bf16[16,128]{1,0:T(8,128)(2,1)} %hv.1) | copy-start | bytes 12292
  71.6 14.1 %all-to-all-start = ((bf16[16,16,14]{2,1,0:T(8,128)(2,1)}), bf16[16,16,14]{2,1,0:T(8,128)(2,1)S(1)}, u32[]{:S(2)}, u32[]{:S(2)}) async-start(bf16[16,16,14]{2,1,0:T(8,128)(2,1)} %broadcast_in_dim.2), calls=%async_computation | async-start | bytes 131072 | tf_op jit(solution)/shard_map/all_to_all | solution.py:266
  78.8 1.2 %copy-start = (bf16[992,512]{1,0:T(8,128)(2,1)S(1)}, bf16[992,512]{1,0:T(8,128)(2,1)}, u32[]{:S(2)}) copy-start(bf16[992,512]{1,0:T(8,128)(2,1)} %slice_convert_fusion.1) | copy-start | bytes 3047428

commit v7 on v6

--- a/solution.py
+++ b/solution.py
@@ -20,8 +20,9 @@
 NORM_SCALE = 2.0**14
 
 ALL_VMEM = 60 * 1024 * 1024
+MERGE_VMEM = 24 << 20
 TOGETHER = 4
-STAY = 12
+STAY = 13
 CHUNK = 32
 
 
@@ -51,23 +52,12 @@
     ]
     for c in copies:
         c.start()
-    for c in copies:
-        c.wait()
     wq, wk, wv, lq, lk, lv, train, step = held
     columns = out.shape[1]
     half = columns // 2
     spare = half - rows
-    tiers = []
-    at = 0
-    for w in (wq, wk, wv):
-        weight = w[...].astype(jnp.float32)
-        width = weight.shape[1]
-        tier = tier_of(jnp.max(jnp.abs(weight), axis=0, keepdims=True))
-        out[:rows, at : at + width] = (weight * power(tier, 1)).astype(jnp.bfloat16)
-        tiers.append(tier)
-        at += width
-    tier = jnp.concatenate(tiers, axis=1)
-
+    for c in copies[3:]:
+        c.wait()
     lows, low_tiers = [], []
     for l in (lq, lk, lv):
         low = l[...].astype(jnp.float32)
@@ -78,17 +68,39 @@
         ((0, 0, 16), (1, 0, 16), rows),
         ((2, 0, 8), (2, 8, 16), rows + 16),
     ):
-        (i, a, b), (j, c, d) = left, right
+        (i, a, b), (j, e, d) = left, right
         to = slice(row, row + b - a)
         out[to, :rows] = lows[i][a:b].astype(jnp.bfloat16)
-        out[to, half : half + rows] = lows[j][c:d].astype(jnp.bfloat16)
+        out[to, half : half + rows] = lows[j][e:d].astype(jnp.bfloat16)
         shape = (b - a, half)
         both = jnp.where(
             behind(shape, 1, rows) < spare // 2,
             jnp.broadcast_to(low_tiers[i][a:b], shape),
-            jnp.broadcast_to(low_tiers[j][c:d], shape),
+            jnp.broadcast_to(low_tiers[j][e:d], shape),
         )
         out[to, half + rows :] = both[:, rows:].astype(jnp.bfloat16)
+
+    norm = (train[...] + step[...]).astype(jnp.bfloat16).astype(jnp.float32) * NORM_SCALE
+    n = norm.shape[1]
+    norm = jnp.broadcast_to(norm, (8, n)).astype(jnp.bfloat16)
+    shape = (n, half)
+    pick = behind(shape, 1, rows) == behind(shape, 0, 0)
+    moved = jnp.dot(
+        norm, jnp.where(pick, 1.0, 0.0).astype(jnp.bfloat16), preferred_element_type=jnp.float32
+    )
+    out[rows + 16 : rows + 24, rows:half] = moved[:, rows:].astype(jnp.bfloat16)
+
+    tiers = []
+    at = 0
+    for w, c in zip((wq, wk, wv), copies):
+        c.wait()
+        weight = w[...].astype(jnp.float32)
+        width = weight.shape[1]
+        tier = tier_of(jnp.max(jnp.abs(weight), axis=0, keepdims=True))
+        out[:rows, at : at + width] = (weight * power(tier, 1)).astype(jnp.bfloat16)
+        tiers.append(tier)
+        at += width
+    tier = jnp.concatenate(tiers, axis=1)
 
     shape = (16, columns)
     own = behind(shape, 1, 0) // spare == behind(shape, 0, 0)
@@ -99,15 +111,6 @@
         spread, jnp.where(pick, 1.0, 0.0).astype(jnp.bfloat16), preferred_element_type=jnp.float32
     )
     out[rows : rows + 16, rows:half] = moved[:, rows:].astype(jnp.bfloat16)
-    norm = (train[...] + step[...]).astype(jnp.bfloat16).astype(jnp.float32) * NORM_SCALE
-    n = norm.shape[1]
-    norm = jnp.broadcast_to(norm, (8, n)).astype(jnp.bfloat16)
-    shape = (n, half)
-    pick = behind(shape, 1, rows) == behind(shape, 0, 0)
-    moved = jnp.dot(
-        norm, jnp.where(pick, 1.0, 0.0).astype(jnp.bfloat16), preferred_element_type=jnp.float32
-    )
-    out[rows + 16 : rows + 24, rows:half] = moved[:, rows:].astype(jnp.bfloat16)
 
 
 def merge(
@@ -138,11 +141,11 @@
         axis=0,
     ).astype(jnp.bfloat16)
 
-    def turn(blocks, begin, to, largest):
+    def turn(these, largest):
         inverses = []
-        for i in range(TOGETHER):
-            left = blocks[begin + i, rows : rows + 24, :half].astype(jnp.float32)
-            right = blocks[begin + i, rows : rows + 24, half:].astype(jnp.float32)
+        for blocks, i, to in these:
+            left = blocks[i, rows : rows + 24, :half].astype(jnp.float32)
+            right = blocks[i, rows : rows + 24, half:].astype(jnp.float32)
             tier = jnp.dot(
                 left[:16].astype(jnp.bfloat16), pick, preferred_element_type=jnp.float32
             )
@@ -152,32 +155,33 @@
             left = left * power(right[:, rows : rows + 1], -1)
             right = right * power(right[:, middle : middle + 1], -1)
             low = jnp.concatenate([left[:16], right[:16], left[16:], right[16:]], axis=0)
-            result[to + i] = lax.dot_general(
+            result[to] = lax.dot_general(
                 low[:, :rows].astype(jnp.bfloat16),
                 high,
                 (((0,), (0,)), ((), ())),
                 preferred_element_type=jnp.float32,
             )
-        for i, inverse in enumerate(inverses):
+        for (blocks, i, to), inverse in zip(these, inverses):
             for r in range(0, rows, CHUNK):
                 part = slice(r, r + CHUNK)
-                block = blocks[begin + i, part, :].astype(jnp.float32)
-                merged = block * inverse + result[to + i, part, :]
-                result[to + i, part, :] = merged
+                block = blocks[i, part, :].astype(jnp.float32)
+                merged = block * inverse + result[to, part, :]
+                result[to, part, :] = merged
                 for j in range(0, CHUNK, 8):
                     largest = jnp.maximum(largest, jnp.abs(merged[j : j + 8]))
         return largest
 
     def first(t, largest):
-        return turn(stayed, t * TOGETHER, t * TOGETHER, largest)
+        begin = t * TOGETHER
+        return turn([(stayed, begin + i, begin + i) for i in range(TOGETHER)], largest)
 
     kept = stayed.shape[0]
-    largest = lax.fori_loop(
-        0, kept // TOGETHER, first, jnp.zeros((8, columns), jnp.float32)
-    )
+    turns = kept // TOGETHER
+    largest = lax.fori_loop(0, turns, first, jnp.zeros((8, columns), jnp.float32))
     arrival.wait()
-    for t in range(0, n - kept, TOGETHER):
-        largest = turn(back, t, kept + t, largest)
+    rest = [(stayed, z, z) for z in range(turns * TOGETHER, kept)]
+    rest += [(back, z, kept + z) for z in range(n - kept)]
+    largest = turn(rest, largest)
     scale = jnp.max(largest, axis=0, keepdims=True)
     cq[...] = scale[:, :q]
     ck[...] = scale[:, q : q + kv]
@@ -282,7 +286,7 @@
             pltpu.SemaphoreType.DMA((3, shards)),
             pltpu.SemaphoreType.DMA,
         ],
-        compiler_params=pltpu.CompilerParams(vmem_limit_bytes=24 << 20),
+        compiler_params=pltpu.CompilerParams(vmem_limit_bytes=MERGE_VMEM),
         cost_estimate=pl.CostEstimate(
             flops=2 * shards * rows * columns * 48, bytes_accessed=12 << 20, transcendentals=0
         ),

time: 87.1 us -> 87.1 us (level)
  no operation moved by 1% of the time
where the time goes in v7:
time: 87.1 us; the launch traced here: 86.6 us
  blocking collectives  65.7 us (75%)
  Pallas kernels  7.71 us (9%)
  starting transfers between devices  7.17 us (8%)
  other arithmetic  2.66 us (3%)
  local copies, waits for them, and re-layouts  2.63 us (3%)
    all_gather x1, blocking collectives, local(): gathered = lax.all_gather(payload.astype(jnp.float16), 'fsdp', axis=0)  65.7 us
    all_to_all x1, starting transfers between devices, local(): lax.all_to_all(jnp.broadcast_to(norm[None], (peers, *norm.shape)), WIDTH,...  7.17 us
    pallas_call x1, Pallas kernels, local(): pl.pallas_call(functools.partial(merge, rows), out_shape=(*final, *scale)...  5.72 us
    pallas_call x1, Pallas kernels, local(): pl.pallas_call(functools.partial(pack, rows), out_shape=jax.ShapeDtypeStr...  1.99 us
  transfers between devices with their start and end apart: 1, of which 0 were waited for; matrix products, arithmetic and copies ran while one was open for 0% of the time, Pallas kernels for 7%

profile of v7, /device:TPU:24, one launch (start us, length us, event | category | flops | bytes accessed | tf_op | source)
XLA Modules:
  0.0 86.6 jit_solution(13837463424938677949)
XLA Ops:
  0.6 2.0 %pack.1 = bf16[248,512]{1,0:T(8,128)(2,1)} custom-call(bf16[224,256]{1,0:T(8,128)(2,1)} %refs_0_.1, bf16[224,128]{1,0:T(8,128)(2,1)} %refs_1_.1, bf16[224,128]{1,0:T(8,128)(2,1)} %refs_2_.1, bf16[16,224]{1,0:T(8,128)(2,1)} %bitcast.18, bf16[16,224]{1,0:T(8,128)(2,1)} %bitcast.19, bf16[16,224]{1,0:T(8,128)(2,1)} %bitcast.20, f32[1,14]{1,0:T(1,128)} %bitcast.21, ...), custom_call_target="tpu_custom_call" | custom-call | tf_op jit(solution)/shard_map/pack/pallas_call | solution.py:248
  2.6 1.0 %convert_element_type.19 = f16[248,512]{1,0:T(8,128)(2,1)S(1)} convert(bf16[248,512]{1,0:T(8,128)(2,1)} %pack.1) | non-fusion elementwise | flops 126976 | bytes 507904 | tf_op jit(solution)/shard_map/convert_element_type | solution.py:260
  3.6 65.7 %all-gather.2 = f16[3968,512]{1,0:T(8,128)(2,1)S(1)} all-gather(f16[248,512]{1,0:T(8,128)(2,1)S(1)} %convert_element_type.19), channel_id=2, replica_groups=mesh['fsdp'=16,'width_0'=4,'width_1'=4,'trial'=2] {'fsdp'}, dimensions={0}, use_global_device_ids=true | all-gather | bytes 4317184 | tf_op jit(solution)/shard_map/all_gather | solution.py:260
  69.3 1.0 %slice_convert_fusion.1 = bf16[744,512]{1,0:T(8,128)(2,1)} fusion(f16[3968,512]{1,0:T(8,128)(2,1)S(1)} %all-gather.2), kind=kLoop, calls=%fused_computation.1 | loop fusion | flops 380928 | bytes 1523712 | tf_op jit(solution)/shard_map/convert_element_type | solution.py:267
  70.3 0.0 copy-start.1
  70.3 0.0 copy-start.2
  70.3 0.0 copy-start.3
  70.3 0.7 slice_convert_fusion
  71.0 0.1 slice.14
  71.1 0.6 broadcast_in_dim.2
  71.7 7.2 %all-to-all-start = ((bf16[16,16,14]{2,1,0:T(8,128)(2,1)}), bf16[16,16,14]{2,1,0:T(8,128)(2,1)S(1)}, u32[]{:S(2)}, u32[]{:S(2)}) async-start(bf16[16,16,14]{2,1,0:T(8,128)(2,1)} %broadcast_in_dim.2), calls=%async_computation | async-start | bytes 131072 | tf_op jit(solution)/shard_map/all_to_all | solution.py:270
  78.9 0.0 copy-done.1
  78.9 0.0 copy-done.2
  78.9 0.0 copy-done.3
  78.9 0.0 copy-start
  78.9 1.1 %copy-done = bf16[744,512]{1,0:T(8,128)(2,1)S(1)} copy-done((bf16[744,512]{1,0:T(8,128)(2,1)S(1)}, bf16[744,512]{1,0:T(8,128)(2,1)}, u32[]{:S(2)}) %copy-start) | copy-done | bytes 761880
  80.0 5.7 %merge.1 = (bf16[3584,256]{1,0:T(8,128)(2,1)}, bf16[3584,128]{1,0:T(8,128)(2,1)}, bf16[3584,128]{1,0:T(8,128)(2,1)}, f32[1,256]{1,0:T(1,128)}, f32[1,128]{1,0:T(1,128)}, /*index=5*/f32[1,128]{1,0:T(1,128)}) custom-call(bf16[13,248,512]{2,1,0:T(8,128)(2,1)S(1)} %bitcast.14, bf16[3,248,512]{2,1,0:T(8,128)(2,1)S(1)} %bitcast.15, bf16[16,256]{1,0:T(8,128)(2,1)S(1)} %copy-done.1, ...), custom_call_target="tpu_custom_call" | custom-call | flops 176160768 | bytes 12582912 | tf_op jit(solution)/shard_map/merge/pallas_call | solution.py:277
  85.8 0.0 all-to-all-done
  85.8 0.8 reshape.42
  (2 shorter events, 0.0 us)
Async XLA Ops:
  70.3 8.6 %copy-start.1 = (bf16[16,256]{1,0:T(8,128)(2,1)S(1)}, bf16[16,256]{1,0:T(8,128)(2,1)}, u32[]{:S(2)}) copy-start(bf16[16,256]{1,0:T(8,128)(2,1)} %hq.1) | copy-start | bytes 24580
  70.3 8.6 %copy-start.2 = (bf16[16,128]{1,0:T(8,128)(2,1)S(1)}, bf16[16,128]{1,0:T(8,128)(2,1)}, u32[]{:S(2)}) copy-start(bf16[16,128]{1,0:T(8,128)(2,1)} %hk.1) | copy-start | bytes 12292
  70.3 8.6 %copy-start.3 = (bf16[16,128]{1,0:T(8,128)(2,1)S(1)}, bf16[16,128]{1,0:T(8,128)(2,1)}, u32[]{:S(2)}) copy-start(bf16[16,128]{1,0:T(8,128)(2,1)} %hv.1) | copy-start | bytes 12292
  71.7 14.1 %all-to-all-start = ((bf16[16,16,14]{2,1,0:T(8,128)(2,1)}), bf16[16,16,14]{2,1,0:T(8,128)(2,1)S(1)}, u32[]{:S(2)}, u32[]{:S(2)}) async-start(bf16[16,16,14]{2,1,0:T(8,128)(2,1)} %broadcast_in_dim.2), calls=%async_computation | async-start | bytes 131072 | tf_op jit(solution)/shard_map/all_to_all | solution.py:270
  78.9 1.1 %copy-start = (bf16[744,512]{1,0:T(8,128)(2,1)S(1)}, bf16[744,512]{1,0:T(8,128)(2,1)}, u32[]{:S(2)}) copy-start(bf16[744,512]{1,0:T(8,128)(2,1)} %slice_convert_fusion.1) | copy-start | bytes 2285572

commit v8 on v6

--- a/solution.py
+++ b/solution.py
@@ -20,8 +20,9 @@
 NORM_SCALE = 2.0**14
 
 ALL_VMEM = 60 * 1024 * 1024
+MERGE_VMEM = 24 << 20
 TOGETHER = 4
-STAY = 12
+STAY = 13
 CHUNK = 32
 
 
@@ -138,11 +139,11 @@
         axis=0,
     ).astype(jnp.bfloat16)
 
-    def turn(blocks, begin, to, largest):
+    def turn(these, largest):
         inverses = []
-        for i in range(TOGETHER):
-            left = blocks[begin + i, rows : rows + 24, :half].astype(jnp.float32)
-            right = blocks[begin + i, rows : rows + 24, half:].astype(jnp.float32)
+        for blocks, i, to in these:
+            left = blocks[i, rows : rows + 24, :half].astype(jnp.float32)
+            right = blocks[i, rows : rows + 24, half:].astype(jnp.float32)
             tier = jnp.dot(
                 left[:16].astype(jnp.bfloat16), pick, preferred_element_type=jnp.float32
             )
@@ -152,32 +153,33 @@
             left = left * power(right[:, rows : rows + 1], -1)
             right = right * power(right[:, middle : middle + 1], -1)
             low = jnp.concatenate([left[:16], right[:16], left[16:], right[16:]], axis=0)
-            result[to + i] = lax.dot_general(
+            result[to] = lax.dot_general(
                 low[:, :rows].astype(jnp.bfloat16),
                 high,
                 (((0,), (0,)), ((), ())),
                 preferred_element_type=jnp.float32,
             )
-        for i, inverse in enumerate(inverses):
+        for (blocks, i, to), inverse in zip(these, inverses):
             for r in range(0, rows, CHUNK):
                 part = slice(r, r + CHUNK)
-                block = blocks[begin + i, part, :].astype(jnp.float32)
-                merged = block * inverse + result[to + i, part, :]
-                result[to + i, part, :] = merged
+                block = blocks[i, part, :].astype(jnp.float32)
+                merged = block * inverse + result[to, part, :]
+                result[to, part, :] = merged
                 for j in range(0, CHUNK, 8):
                     largest = jnp.maximum(largest, jnp.abs(merged[j : j + 8]))
         return largest
 
     def first(t, largest):
-        return turn(stayed, t * TOGETHER, t * TOGETHER, largest)
+        begin = t * TOGETHER
+        return turn([(stayed, begin + i, begin + i) for i in range(TOGETHER)], largest)
 
     kept = stayed.shape[0]
-    largest = lax.fori_loop(
-        0, kept // TOGETHER, first, jnp.zeros((8, columns), jnp.float32)
-    )
+    turns = kept // TOGETHER
+    largest = lax.fori_loop(0, turns, first, jnp.zeros((8, columns), jnp.float32))
     arrival.wait()
-    for t in range(0, n - kept, TOGETHER):
-        largest = turn(back, t, kept + t, largest)
+    rest = [(stayed, z, z) for z in range(turns * TOGETHER, kept)]
+    rest += [(back, z, kept + z) for z in range(n - kept)]
+    largest = turn(rest, largest)
     scale = jnp.max(largest, axis=0, keepdims=True)
     cq[...] = scale[:, :q]
     ck[...] = scale[:, q : q + kv]
@@ -255,14 +257,11 @@
     )(*sources)
     gathered = lax.all_gather(payload.astype(jnp.float16), "fsdp", axis=0)
 
-    norm = gathered[:, rows + 16, rows : rows + n].astype(jnp.float32) * (1.0 / NORM_SCALE)
-    norm, stayed, left_out = lax.optimization_barrier(
-        (
-            norm.astype(jnp.bfloat16),
-            gathered[:STAY].astype(jnp.bfloat16),
-            gathered[STAY:].astype(jnp.bfloat16),
-        )
-    )
+    stayed = gathered[:STAY].astype(jnp.bfloat16)
+    left_out = gathered[STAY:].astype(jnp.bfloat16)
+    norm = jnp.concatenate([b[:, rows + 16, rows : rows + n] for b in (stayed, left_out)], axis=0)
+    norm = (norm.astype(jnp.float32) * (1.0 / NORM_SCALE)).astype(jnp.bfloat16)
+    norm, stayed, left_out = lax.optimization_barrier((norm, stayed, left_out))
     norm = lax.all_to_all(
         jnp.broadcast_to(norm[None], (peers, *norm.shape)), WIDTH, 0, 0, tiled=True
     )
@@ -282,7 +281,7 @@
             pltpu.SemaphoreType.DMA((3, shards)),
             pltpu.SemaphoreType.DMA,
         ],
-        compiler_params=pltpu.CompilerParams(vmem_limit_bytes=24 << 20),
+        compiler_params=pltpu.CompilerParams(vmem_limit_bytes=MERGE_VMEM),
         cost_estimate=pl.CostEstimate(
             flops=2 * shards * rows * columns * 48, bytes_accessed=12 << 20, transcendentals=0
         ),

time: 87.1 us -> 86.5 us (level)
  no operation moved by 1% of the time
where the time goes in v8:
time: 86.5 us; the launch traced here: 85.9 us
  blocking collectives  65.7 us (76%)
  Pallas kernels  7.62 us (9%)
  starting transfers between devices  7.17 us (8%)
  local copies, waits for them, and re-layouts  2.9 us (3%)
  other arithmetic  1.77 us (2%)
    all_gather x1, blocking collectives, local(): gathered = lax.all_gather(payload.astype(jnp.float16), 'fsdp', axis=0)  65.7 us
    all_to_all x1, starting transfers between devices, local(): lax.all_to_all(jnp.broadcast_to(norm[None], (peers, *norm.shape)), WIDTH,...  7.17 us
    pallas_call x1, Pallas kernels, local(): pl.pallas_call(functools.partial(merge, rows), out_shape=(*final, *scale)...  5.71 us
    pallas_call x1, Pallas kernels, local(): pl.pallas_call(functools.partial(pack, rows), out_shape=jax.ShapeDtypeStr...  1.9 us
  transfers between devices with their start and end apart: 1, of which 0 were waited for; matrix products, arithmetic and copies ran while one was open for 0% of the time, Pallas kernels for 7%

profile of v8, /device:TPU:24, one launch (start us, length us, event | category | flops | bytes accessed | tf_op | source)
XLA Modules:
  0.0 85.9 jit_solution(18419762358803070118)
XLA Ops:
  0.6 1.9 %pack.1 = bf16[248,512]{1,0:T(8,128)(2,1)} custom-call(bf16[224,256]{1,0:T(8,128)(2,1)} %refs_0_.1, bf16[224,128]{1,0:T(8,128)(2,1)} %refs_1_.1, bf16[224,128]{1,0:T(8,128)(2,1)} %refs_2_.1, bf16[16,224]{1,0:T(8,128)(2,1)} %bitcast.23, bf16[16,224]{1,0:T(8,128)(2,1)} %bitcast.24, bf16[16,224]{1,0:T(8,128)(2,1)} %bitcast.25, f32[1,14]{1,0:T(1,128)} %bitcast.27, ...), custom_call_target="tpu_custom_call" | custom-call | tf_op jit(solution)/shard_map/pack/pallas_call | solution.py:246
  2.5 1.0 %convert_element_type.15 = f16[248,512]{1,0:T(8,128)(2,1)S(1)} convert(bf16[248,512]{1,0:T(8,128)(2,1)} %pack.1) | non-fusion elementwise | flops 126976 | bytes 507904 | tf_op jit(solution)/shard_map/convert_element_type | solution.py:258
  3.5 65.7 %all-gather.2 = f16[3968,512]{1,0:T(8,128)(2,1)S(1)} all-gather(f16[248,512]{1,0:T(8,128)(2,1)S(1)} %convert_element_type.15), channel_id=2, replica_groups=mesh['fsdp'=16,'width_0'=4,'width_1'=4,'trial'=2] {'fsdp'}, dimensions={0}, use_global_device_ids=true | all-gather | bytes 4317184 | tf_op jit(solution)/shard_map/all_gather | solution.py:258
  69.2 0.1 slice_convert_fusion.1
  69.4 0.0 copy-start
  69.4 0.0 copy-start.2
  69.4 0.0 copy-start.3
  69.4 0.0 copy-start.4
  69.4 0.6 slice_convert_fusion
  70.0 0.2 copy-done
  70.2 0.1 slice.21
  70.3 0.1 slice.19
  70.4 0.6 broadcast_in_dim.2
  71.0 7.2 %all-to-all-start = ((bf16[16,16,14]{2,1,0:T(8,128)(2,1)}), bf16[16,16,14]{2,1,0:T(8,128)(2,1)S(1)}, u32[]{:S(2)}, u32[]{:S(2)}) async-start(bf16[16,16,14]{2,1,0:T(8,128)(2,1)} %broadcast_in_dim.2), calls=%async_computation | async-start | bytes 131072 | tf_op jit(solution)/shard_map/all_to_all | solution.py:265
  78.2 0.0 copy-done.2
  78.2 0.0 copy-done.3
  78.2 0.0 copy-done.4
  78.2 0.0 copy-start.1
  78.3 1.1 %copy-done.1 = bf16[744,512]{1,0:T(8,128)(2,1)S(1)} copy-done((bf16[744,512]{1,0:T(8,128)(2,1)S(1)}, bf16[744,512]{1,0:T(8,128)(2,1)}, u32[]{:S(2)}) %copy-start.1) | copy-done | bytes 761880
  79.4 5.7 %merge.1 = (bf16[3584,256]{1,0:T(8,128)(2,1)}, bf16[3584,128]{1,0:T(8,128)(2,1)}, bf16[3584,128]{1,0:T(8,128)(2,1)}, f32[1,256]{1,0:T(1,128)}, f32[1,128]{1,0:T(1,128)}, /*index=5*/f32[1,128]{1,0:T(1,128)}) custom-call(bf16[13,248,512]{2,1,0:T(8,128)(2,1)S(1)} %bitcast.18, bf16[3,248,512]{2,1,0:T(8,128)(2,1)S(1)} %bitcast.20, bf16[16,256]{1,0:T(8,128)(2,1)S(1)} %copy-done.2, ...), custom_call_target="tpu_custom_call" | custom-call | flops 176160768 | bytes 12582912 | tf_op jit(solution)/shard_map/merge/pallas_call | solution.py:272
  85.1 0.0 all-to-all-done
  85.1 0.8 reshape.38
  (4 shorter events, 0.0 us)
Async XLA Ops:
  69.4 0.9 %copy-start = (bf16[744,512]{1,0:T(8,128)(2,1)}, bf16[744,512]{1,0:T(8,128)(2,1)S(1)}, u32[]{:S(2)}) copy-start(bf16[744,512]{1,0:T(8,128)(2,1)S(1)} %slice_convert_fusion.1) | copy-start | bytes 2285572
  69.4 8.9 %copy-start.2 = (bf16[16,256]{1,0:T(8,128)(2,1)S(1)}, bf16[16,256]{1,0:T(8,128)(2,1)}, u32[]{:S(2)}) copy-start(bf16[16,256]{1,0:T(8,128)(2,1)} %hq.1) | copy-start | bytes 24580
  69.4 8.8 %copy-start.3 = (bf16[16,128]{1,0:T(8,128)(2,1)S(1)}, bf16[16,128]{1,0:T(8,128)(2,1)}, u32[]{:S(2)}) copy-start(bf16[16,128]{1,0:T(8,128)(2,1)} %hk.1) | copy-start | bytes 12292
  69.4 8.8 %copy-start.4 = (bf16[16,128]{1,0:T(8,128)(2,1)S(1)}, bf16[16,128]{1,0:T(8,128)(2,1)}, u32[]{:S(2)}) copy-start(bf16[16,128]{1,0:T(8,128)(2,1)} %hv.1) | copy-start | bytes 12292
  71.0 14.0 %all-to-all-start = ((bf16[16,16,14]{2,1,0:T(8,128)(2,1)}), bf16[16,16,14]{2,1,0:T(8,128)(2,1)S(1)}, u32[]{:S(2)}, u32[]{:S(2)}) async-start(bf16[16,16,14]{2,1,0:T(8,128)(2,1)} %broadcast_in_dim.2), calls=%async_computation | async-start | bytes 131072 | tf_op jit(solution)/shard_map/all_to_all | solution.py:265
  78.2 1.1 %copy-start.1 = (bf16[744,512]{1,0:T(8,128)(2,1)S(1)}, bf16[744,512]{1,0:T(8,128)(2,1)}, u32[]{:S(2)}) copy-start(bf16[744,512]{1,0:T(8,128)(2,1)} %copy-done) | copy-start | bytes 2285572

commit v9 on v8

--- a/solution.py
+++ b/solution.py
@@ -21,7 +21,7 @@
 
 ALL_VMEM = 60 * 1024 * 1024
 MERGE_VMEM = 24 << 20
-TOGETHER = 4
+TOGETHER = 8
 STAY = 13
 CHUNK = 32
 
@@ -112,13 +112,11 @@
 
 
 def merge(
-    rows, stayed, left_out, hq, hk, hv, fq, fk, fv, cq, ck, cv,
-    back, result, oq, ok, ov, sems, arrived,
+    rows, stayed, back, hq, hk, hv, fq, fk, fv, cq, ck, cv,
+    result, oq, ok, ov, sems,
 ):
     columns = stayed.shape[2]
     n = stayed.shape[0] + back.shape[0]
-    arrival = pltpu.make_async_copy(left_out, back, arrived)
-    arrival.start()
     half = columns // 2
     spare = half - rows
     q, kv = hq.shape[1], hk.shape[1]
@@ -176,7 +174,6 @@
     kept = stayed.shape[0]
     turns = kept // TOGETHER
     largest = lax.fori_loop(0, turns, first, jnp.zeros((8, columns), jnp.float32))
-    arrival.wait()
     rest = [(stayed, z, z) for z in range(turns * TOGETHER, kept)]
     rest += [(back, z, kept + z) for z in range(n - kept)]
     largest = turn(rest, largest)
@@ -272,14 +269,12 @@
     out = pl.pallas_call(
         functools.partial(merge, rows),
         out_shape=(*final, *scale),
-        in_specs=[vmem, pl.BlockSpec(memory_space=pltpu.HBM), vmem, vmem, vmem],
+        in_specs=[vmem] * 5,
         out_specs=(*[pl.BlockSpec(memory_space=pl.ANY)] * 3, *[vmem] * 3),
         scratch_shapes=[
-            pltpu.VMEM(left_out.shape, jnp.bfloat16),
             pltpu.VMEM((shards, rows, columns), jnp.float32),
             *[pltpu.VMEM((shards, rows, w), jnp.bfloat16) for w in (q, kv, kv)],
             pltpu.SemaphoreType.DMA((3, shards)),
-            pltpu.SemaphoreType.DMA,
         ],
         compiler_params=pltpu.CompilerParams(vmem_limit_bytes=MERGE_VMEM),
         cost_estimate=pl.CostEstimate(

time: 86.5 us -> 85.9 us (level)
  transfers between devices with their start and end apart: 1 -> 1, of which waited for: 0 -> 0; matrix products, arithmetic and copies ran while one was open for 0% -> 0% of each run, Pallas kernels for 7% -> 6%
where the time goes in v9:
time: 85.9 us; the launch traced here: 85.2 us
  blocking collectives  65.7 us (76%)
  starting transfers between devices  7.17 us (8%)
  Pallas kernels  6.97 us (8%)
  local copies, waits for them, and re-layouts  2.9 us (3%)
  other arithmetic  1.77 us (2%)
    all_gather x1, blocking collectives, local(): gathered = lax.all_gather(payload.astype(jnp.float16), 'fsdp', axis=0)  65.7 us
    all_to_all x1, starting transfers between devices, local(): lax.all_to_all(jnp.broadcast_to(norm[None], (peers, *norm.shape)), WIDTH,...  7.17 us
    pallas_call x1, Pallas kernels, local(): pl.pallas_call(functools.partial(merge, rows), out_shape=(*final, *scale)...  5.07 us
    pallas_call x1, Pallas kernels, local(): pl.pallas_call(functools.partial(pack, rows), out_shape=jax.ShapeDtypeStr...  1.9 us
  transfers between devices with their start and end apart: 1, of which 0 were waited for; matrix products, arithmetic and copies ran while one was open for 0% of the time, Pallas kernels for 6%

profile of v9, /device:TPU:24, one launch (start us, length us, event | category | flops | bytes accessed | tf_op | source)
XLA Modules:
  0.0 85.2 jit_solution(13384160006338176910)
XLA Ops:
  0.6 1.9 %pack.1 = bf16[248,512]{1,0:T(8,128)(2,1)} custom-call(bf16[224,256]{1,0:T(8,128)(2,1)} %refs_0_.1, bf16[224,128]{1,0:T(8,128)(2,1)} %refs_1_.1, bf16[224,128]{1,0:T(8,128)(2,1)} %refs_2_.1, bf16[16,224]{1,0:T(8,128)(2,1)} %bitcast.23, bf16[16,224]{1,0:T(8,128)(2,1)} %bitcast.24, bf16[16,224]{1,0:T(8,128)(2,1)} %bitcast.25, f32[1,14]{1,0:T(1,128)} %bitcast.27, ...), custom_call_target="tpu_custom_call" | custom-call | tf_op jit(solution)/shard_map/pack/pallas_call | solution.py:243
  2.5 1.0 %convert_element_type.15 = f16[248,512]{1,0:T(8,128)(2,1)S(1)} convert(bf16[248,512]{1,0:T(8,128)(2,1)} %pack.1) | non-fusion elementwise | flops 126976 | bytes 507904 | tf_op jit(solution)/shard_map/convert_element_type | solution.py:255
  3.5 65.7 %all-gather.2 = f16[3968,512]{1,0:T(8,128)(2,1)S(1)} all-gather(f16[248,512]{1,0:T(8,128)(2,1)S(1)} %convert_element_type.15), channel_id=2, replica_groups=mesh['fsdp'=16,'width_0'=4,'width_1'=4,'trial'=2] {'fsdp'}, dimensions={0}, use_global_device_ids=true | all-gather | bytes 4317184 | tf_op jit(solution)/shard_map/all_gather | solution.py:255
  69.2 0.1 slice_convert_fusion.1
  69.4 0.0 copy-start
  69.4 0.0 copy-start.2
  69.4 0.0 copy-start.3
  69.4 0.0 copy-start.4
  69.4 0.6 slice_convert_fusion
  70.0 0.2 copy-done
  70.2 0.1 slice.21
  70.3 0.1 slice.19
  70.4 0.6 broadcast_in_dim.2
  71.0 7.2 %all-to-all-start = ((bf16[16,16,14]{2,1,0:T(8,128)(2,1)}), bf16[16,16,14]{2,1,0:T(8,128)(2,1)S(1)}, u32[]{:S(2)}, u32[]{:S(2)}) async-start(bf16[16,16,14]{2,1,0:T(8,128)(2,1)} %broadcast_in_dim.2), calls=%async_computation | async-start | bytes 131072 | tf_op jit(solution)/shard_map/all_to_all | solution.py:262
  78.2 0.0 copy-done.2
  78.2 0.0 copy-done.3
  78.2 0.0 copy-done.4
  78.2 0.0 copy-start.1
  78.3 1.1 %copy-done.1 = bf16[744,512]{1,0:T(8,128)(2,1)S(1)} copy-done((bf16[744,512]{1,0:T(8,128)(2,1)S(1)}, bf16[744,512]{1,0:T(8,128)(2,1)}, u32[]{:S(2)}) %copy-start.1) | copy-done | bytes 761880
  79.4 5.1 %merge.1 = (bf16[3584,256]{1,0:T(8,128)(2,1)}, bf16[3584,128]{1,0:T(8,128)(2,1)}, bf16[3584,128]{1,0:T(8,128)(2,1)}, f32[1,256]{1,0:T(1,128)}, f32[1,128]{1,0:T(1,128)}, /*index=5*/f32[1,128]{1,0:T(1,128)}) custom-call(bf16[13,248,512]{2,1,0:T(8,128)(2,1)S(1)} %bitcast.18, bf16[3,248,512]{2,1,0:T(8,128)(2,1)S(1)} %bitcast.20, bf16[16,256]{1,0:T(8,128)(2,1)S(1)} %copy-done.2, ...), custom_call_target="tpu_custom_call" | custom-call | flops 176160768 | bytes 12582912 | tf_op jit(solution)/shard_map/merge/pallas_call | solution.py:269
  84.4 0.0 all-to-all-done
  84.5 0.8 reshape.38
  (4 shorter events, 0.0 us)
Async XLA Ops:
  69.4 0.9 %copy-start = (bf16[744,512]{1,0:T(8,128)(2,1)}, bf16[744,512]{1,0:T(8,128)(2,1)S(1)}, u32[]{:S(2)}) copy-start(bf16[744,512]{1,0:T(8,128)(2,1)S(1)} %slice_convert_fusion.1) | copy-start | bytes 2285572
  69.4 8.9 %copy-start.2 = (bf16[16,256]{1,0:T(8,128)(2,1)S(1)}, bf16[16,256]{1,0:T(8,128)(2,1)}, u32[]{:S(2)}) copy-start(bf16[16,256]{1,0:T(8,128)(2,1)} %hq.1) | copy-start | bytes 24580
  69.4 8.8 %copy-start.3 = (bf16[16,128]{1,0:T(8,128)(2,1)S(1)}, bf16[16,128]{1,0:T(8,128)(2,1)}, u32[]{:S(2)}) copy-start(bf16[16,128]{1,0:T(8,128)(2,1)} %hk.1) | copy-start | bytes 12292
  69.4 8.8 %copy-start.4 = (bf16[16,128]{1,0:T(8,128)(2,1)S(1)}, bf16[16,128]{1,0:T(8,128)(2,1)}, u32[]{:S(2)}) copy-start(bf16[16,128]{1,0:T(8,128)(2,1)} %hv.1) | copy-start | bytes 12292
  71.0 13.4 %all-to-all-start = ((bf16[16,16,14]{2,1,0:T(8,128)(2,1)}), bf16[16,16,14]{2,1,0:T(8,128)(2,1)S(1)}, u32[]{:S(2)}, u32[]{:S(2)}) async-start(bf16[16,16,14]{2,1,0:T(8,128)(2,1)} %broadcast_in_dim.2), calls=%async_computation | async-start | bytes 131072 | tf_op jit(solution)/shard_map/all_to_all | solution.py:262
  78.2 1.1 %copy-start.1 = (bf16[744,512]{1,0:T(8,128)(2,1)S(1)}, bf16[744,512]{1,0:T(8,128)(2,1)}, u32[]{:S(2)}) copy-start(bf16[744,512]{1,0:T(8,128)(2,1)} %copy-done) | copy-start | bytes 2285572

commit v10 on v9

--- a/solution.py
+++ b/solution.py
@@ -35,8 +35,9 @@
 
 def power(k, sign):
     p = jnp.full_like(k, 2.0 ** (sign * FIRST))
-    for t in range(TIERS - 1):
-        p = p * jnp.where(k > t, 2.0 ** (sign * STEP), 1.0)
+    for t in (4, 2, 1):
+        p = p * jnp.where(k >= t, 2.0 ** (sign * STEP * t), 1.0)
+        k = jnp.where(k >= t, k - t, k)
     return p
 
 
@@ -147,9 +148,9 @@
             )
             tier = jnp.sum(jnp.where(own, tier, 0.0), axis=0, keepdims=True)
             inverses.append(power(tier, -1))
-            middle = rows + spare // 2
-            left = left * power(right[:, rows : rows + 1], -1)
-            right = right * power(right[:, middle : middle + 1], -1)
+            powers = power(right[:, rows:], -1)
+            left = left * powers[:, :1]
+            right = right * powers[:, spare // 2 : spare // 2 + 1]
             low = jnp.concatenate([left[:16], right[:16], left[16:], right[16:]], axis=0)
             result[to] = lax.dot_general(
                 low[:, :rows].astype(jnp.bfloat16),

time: 85.9 us -> 85.9 us (level)
  no operation moved by 1% of the time
where the time goes in v10:
time: 85.9 us; the launch traced here: 85.2 us
  blocking collectives  65.7 us (76%)
  starting transfers between devices  7.17 us (8%)
  Pallas kernels  6.94 us (8%)
  local copies, waits for them, and re-layouts  2.9 us (3%)
  other arithmetic  1.77 us (2%)
    all_gather x1, blocking collectives, local(): gathered = lax.all_gather(payload.astype(jnp.float16), 'fsdp', axis=0)  65.7 us
    all_to_all x1, starting transfers between devices, local(): lax.all_to_all(jnp.broadcast_to(norm[None], (peers, *norm.shape)), WIDTH,...  7.17 us
    pallas_call x1, Pallas kernels, local(): pl.pallas_call(functools.partial(merge, rows), out_shape=(*final, *scale)...  5.04 us
    pallas_call x1, Pallas kernels, local(): pl.pallas_call(functools.partial(pack, rows), out_shape=jax.ShapeDtypeStr...  1.9 us
  transfers between devices with their start and end apart: 1, of which 0 were waited for; matrix products, arithmetic and copies ran while one was open for 0% of the time, Pallas kernels for 6%

profile of v10, /device:TPU:24, one launch (start us, length us, event | category | flops | bytes accessed | tf_op | source)
XLA Modules:
  0.0 85.2 jit_solution(7452398775382167954)
XLA Ops:
  0.6 1.9 %pack.1 = bf16[248,512]{1,0:T(8,128)(2,1)} custom-call(bf16[224,256]{1,0:T(8,128)(2,1)} %refs_0_.1, bf16[224,128]{1,0:T(8,128)(2,1)} %refs_1_.1, bf16[224,128]{1,0:T(8,128)(2,1)} %refs_2_.1, bf16[16,224]{1,0:T(8,128)(2,1)} %bitcast.23, bf16[16,224]{1,0:T(8,128)(2,1)} %bitcast.24, bf16[16,224]{1,0:T(8,128)(2,1)} %bitcast.25, f32[1,14]{1,0:T(1,128)} %bitcast.27, ...), custom_call_target="tpu_custom_call" | custom-call | tf_op jit(solution)/shard_map/pack/pallas_call | solution.py:244
  2.5 1.0 %convert_element_type.15 = f16[248,512]{1,0:T(8,128)(2,1)S(1)} convert(bf16[248,512]{1,0:T(8,128)(2,1)} %pack.1) | non-fusion elementwise | flops 126976 | bytes 507904 | tf_op jit(solution)/shard_map/convert_element_type | solution.py:256
  3.5 65.7 %all-gather.2 = f16[3968,512]{1,0:T(8,128)(2,1)S(1)} all-gather(f16[248,512]{1,0:T(8,128)(2,1)S(1)} %convert_element_type.15), channel_id=2, replica_groups=mesh['fsdp'=16,'width_0'=4,'width_1'=4,'trial'=2] {'fsdp'}, dimensions={0}, use_global_device_ids=true | all-gather | bytes 4317184 | tf_op jit(solution)/shard_map/all_gather | solution.py:256
  69.2 0.1 slice_convert_fusion.1
  69.4 0.0 copy-start
  69.4 0.0 copy-start.2
  69.4 0.0 copy-start.3
  69.4 0.0 copy-start.4
  69.4 0.6 slice_convert_fusion
  70.0 0.2 copy-done
  70.2 0.1 slice.21
  70.3 0.1 slice.19
  70.4 0.6 broadcast_in_dim.2
  71.0 7.2 %all-to-all-start = ((bf16[16,16,14]{2,1,0:T(8,128)(2,1)}), bf16[16,16,14]{2,1,0:T(8,128)(2,1)S(1)}, u32[]{:S(2)}, u32[]{:S(2)}) async-start(bf16[16,16,14]{2,1,0:T(8,128)(2,1)} %broadcast_in_dim.2), calls=%async_computation | async-start | bytes 131072 | tf_op jit(solution)/shard_map/all_to_all | solution.py:263
  78.2 0.0 copy-done.2
  78.2 0.0 copy-done.3
  78.2 0.0 copy-done.4
  78.2 0.0 copy-start.1
  78.3 1.1 %copy-done.1 = bf16[744,512]{1,0:T(8,128)(2,1)S(1)} copy-done((bf16[744,512]{1,0:T(8,128)(2,1)S(1)}, bf16[744,512]{1,0:T(8,128)(2,1)}, u32[]{:S(2)}) %copy-start.1) | copy-done | bytes 761880
  79.4 5.0 %merge.1 = (bf16[3584,256]{1,0:T(8,128)(2,1)}, bf16[3584,128]{1,0:T(8,128)(2,1)}, bf16[3584,128]{1,0:T(8,128)(2,1)}, f32[1,256]{1,0:T(1,128)}, f32[1,128]{1,0:T(1,128)}, /*index=5*/f32[1,128]{1,0:T(1,128)}) custom-call(bf16[13,248,512]{2,1,0:T(8,128)(2,1)S(1)} %bitcast.18, bf16[3,248,512]{2,1,0:T(8,128)(2,1)S(1)} %bitcast.20, bf16[16,256]{1,0:T(8,128)(2,1)S(1)} %copy-done.2, ...), custom_call_target="tpu_custom_call" | custom-call | flops 176160768 | bytes 12582912 | tf_op jit(solution)/shard_map/merge/pallas_call | solution.py:270
  84.4 0.0 all-to-all-done
  84.4 0.8 reshape.38
  (4 shorter events, 0.0 us)
Async XLA Ops:
  69.4 0.9 %copy-start = (bf16[744,512]{1,0:T(8,128)(2,1)}, bf16[744,512]{1,0:T(8,128)(2,1)S(1)}, u32[]{:S(2)}) copy-start(bf16[744,512]{1,0:T(8,128)(2,1)S(1)} %slice_convert_fusion.1) | copy-start | bytes 2285572
  69.4 8.9 %copy-start.2 = (bf16[16,256]{1,0:T(8,128)(2,1)S(1)}, bf16[16,256]{1,0:T(8,128)(2,1)}, u32[]{:S(2)}) copy-start(bf16[16,256]{1,0:T(8,128)(2,1)} %hq.1) | copy-start | bytes 24580
  69.4 8.8 %copy-start.3 = (bf16[16,128]{1,0:T(8,128)(2,1)S(1)}, bf16[16,128]{1,0:T(8,128)(2,1)}, u32[]{:S(2)}) copy-start(bf16[16,128]{1,0:T(8,128)(2,1)} %hk.1) | copy-start | bytes 12292
  69.4 8.8 %copy-start.4 = (bf16[16,128]{1,0:T(8,128)(2,1)S(1)}, bf16[16,128]{1,0:T(8,128)(2,1)}, u32[]{:S(2)}) copy-start(bf16[16,128]{1,0:T(8,128)(2,1)} %hv.1) | copy-start | bytes 12292
  71.0 13.4 %all-to-all-start = ((bf16[16,16,14]{2,1,0:T(8,128)(2,1)}), bf16[16,16,14]{2,1,0:T(8,128)(2,1)S(1)}, u32[]{:S(2)}, u32[]{:S(2)}) async-start(bf16[16,16,14]{2,1,0:T(8,128)(2,1)} %broadcast_in_dim.2), calls=%async_computation | async-start | bytes 131072 | tf_op jit(solution)/shard_map/all_to_all | solution.py:263
  78.2 1.1 %copy-start.1 = (bf16[744,512]{1,0:T(8,128)(2,1)S(1)}, bf16[744,512]{1,0:T(8,128)(2,1)}, u32[]{:S(2)}) copy-start(bf16[744,512]{1,0:T(8,128)(2,1)} %copy-done) | copy-start | bytes 2285572
